TPU v7x, 32 devices: a whole 2x2x4 slice. The times are simulated.
32 devices in a mesh: dp: 2 (over core), seq: 16 (over z, y, x).
Axes of the slice: x: 2, y: 2, z: 4, core: 2. Of those that a mesh axis runs over, the one named last changes fastest.
Arguments:
- hidden: bfloat16 [4, 2, 1024, 2048], P(None, 'dp', 'seq'), may hold values from -6 to 6
- prefix_lengths: int32 [4, 2], replicated, may hold values from 0 to 1023
- cotangent: bfloat16 [4, 2, 1024, 2048], P(None, 'dp', 'seq'), may hold values from -6 to 6
- first_gain: bfloat16 [2048], P(('dp', 'seq')), may hold values from 0.5 to 1.5
- first_shift: bfloat16 [2048], P(('dp', 'seq')), may hold values from -1.5 to 1.5
- triple_weight: bfloat16 [2048, 16, 3, 128], P('seq', 'dp'), may hold values from -0.125 to 0.125
- pair_bias: bfloat16 [4096], P(('dp', 'seq')), may hold values from -1.5 to 1.5
- dense_weight: bfloat16 [2048, 2048], P(('dp', 'seq')), may hold values from -0.375 to 0.375
- dense_shift: bfloat16 [2048], P(('dp', 'seq')), may hold values from -1.5 to 1.5
- second_gain: bfloat16 [2048], P(('dp', 'seq')), may hold values from 0.5 to 1.5
- second_shift: bfloat16 [2048], P(('dp', 'seq')), may hold values from -1.5 to 1.5
- expand_weight: bfloat16 [2048, 8192], P('seq', 'dp'), may hold values from -0.125 to 0.125
- expand_shift: bfloat16 [8192], P(('dp', 'seq')), may hold values from -1.5 to 1.5
- shrink_weight: bfloat16 [8192, 2048], P(('dp', 'seq')), may hold values from -0.09375 to 0.09375
- shrink_shift: bfloat16 [2048], P(('dp', 'seq')), may hold values from -1.5 to 1.5
Outputs:
- layer_output: bfloat16 [4, 2, 1024, 2048], P(None, 'dp', 'seq')
- hidden_grad: bfloat16 [4, 2, 1024, 2048], P(None, 'dp', 'seq')
- first_gain_grad: float32 [2048], P(('dp', 'seq'))
- first_shift_grad: float32 [2048], P(('dp', 'seq'))
- triple_weight_grad: float32 [2048, 16, 3, 128], P('seq', 'dp')
- pair_bias_grad: float32 [4096], P(('dp', 'seq'))
- dense_weight_grad: float32 [2048, 2048], P(('dp', 'seq'))
- dense_shift_grad: float32 [2048], P(('dp', 'seq'))
- second_gain_grad: float32 [2048], P(('dp', 'seq'))
- second_shift_grad: float32 [2048], P(('dp', 'seq'))
- expand_weight_grad: float32 [2048, 8192], P('seq', 'dp')
- expand_shift_grad: float32 [8192], P(('dp', 'seq'))
- shrink_weight_grad: float32 [8192, 2048], P(('dp', 'seq'))
- shrink_shift_grad: float32 [2048], P(('dp', 'seq'))
All inputs are finite; a program needn't handle non-finite values.
Results may differ from a plain program's by a relative error of at most 0.017.
Values may be sent and summed in bfloat16 or wider, within the bound.
A program may use at most 320 MiB of HBM per device.

v0:
```python
import math

import jax
import jax.numpy as jnp
from jax import lax
from jax.sharding import PartitionSpec as P

EPSILON = 1e-05
GELU_SCALE = 0.7978845608028654


def layer_norm(inputs, norm_gain, norm_shift):
    centered = inputs - jnp.mean(inputs, -1, keepdims=True)
    variance = jnp.mean(centered * centered, -1, keepdims=True)
    return centered * lax.rsqrt(variance + EPSILON) * norm_gain + norm_shift


def gelu_tanh(values):
    return (
        0.5 * values * (1.0 + jnp.tanh(GELU_SCALE * (values + 0.044715 * values * values * values)))
    )


def split_norm(inputs, gain_rows, shift_rows):
    return layer_norm(inputs, gain_rows[None, :, None, :], shift_rows[None, :, None, :])


def place_half(values, half_index, group_count):
    chosen = (jnp.arange(group_count, dtype=jnp.int32) == half_index).astype(values.dtype)
    return (chosen[:, None] * values.reshape(1, -1)).reshape(-1)


def shards(
    hidden,
    prefix_lengths,
    cotangent,
    first_gain,
    first_shift,
    triple_weight,
    pair_bias,
    dense_weight,
    dense_shift,
    second_gain,
    second_shift,
    expand_weight,
    expand_shift,
    shrink_weight,
    shrink_shift,
):
    wide_type = jnp.float32
    half_type = jnp.bfloat16
    seq_count = lax.axis_size("seq")
    group_count = lax.axis_size("dp")
    dp_index = lax.axis_index("dp")
    seq_index = lax.axis_index("seq")
    micro_count = hidden.shape[0]
    seq_rows = hidden.shape[2]
    model_width = hidden.shape[3]
    seq_length = seq_rows * seq_count
    local_heads = triple_weight.shape[1]
    head_dim = triple_weight.shape[3]
    head_total = local_heads * group_count
    pair_local = micro_count * group_count * local_heads // seq_count
    unit_local = expand_weight.shape[1]
    project_width = 3 * local_heads * head_dim
    token_total = micro_count * group_count * seq_rows
    score_scale = 1.0 / math.sqrt(head_dim)
    block_rows = min(512, seq_length)
    block_count = seq_length // block_rows
    key_pos = jnp.arange(seq_length, dtype=jnp.int32)
    gathered = (
        lax.all_gather(triple_weight, "seq", axis=0, tiled=True),
        lax.all_gather(dense_weight, "seq", axis=0, tiled=True),
        lax.all_gather(expand_weight, "seq", axis=0, tiled=True),
        lax.all_gather(shrink_weight, "seq", axis=0, tiled=True),
        lax.all_gather(first_gain, "seq", axis=0, tiled=True),
        lax.all_gather(first_shift, "seq", axis=0, tiled=True),
        lax.all_gather(pair_bias, "seq", axis=0, tiled=True),
        lax.all_gather(dense_shift, "seq", axis=0, tiled=True),
        lax.all_gather(second_gain, "seq", axis=0, tiled=True),
        lax.all_gather(second_shift, "seq", axis=0, tiled=True),
        lax.all_gather(expand_shift, "seq", axis=0, tiled=True),
        lax.all_gather(shrink_shift, "seq", axis=0, tiled=True),
    )
    triple_full, dense_full, expand_full, shrink_full = (
        gathered[0],
        gathered[1],
        gathered[2],
        gathered[3],
    )
    row_sets = (
        lax.all_gather(hidden, "dp", axis=1, tiled=True),
        lax.all_gather(cotangent, "dp", axis=1, tiled=True),
        lax.all_gather(gathered[4], "dp", axis=0, tiled=True),
        lax.all_gather(gathered[5], "dp", axis=0, tiled=True),
        lax.all_gather(gathered[6], "dp", axis=0, tiled=True),
        lax.all_gather(gathered[7], "dp", axis=0, tiled=True),
        lax.all_gather(gathered[8], "dp", axis=0, tiled=True),
        lax.all_gather(gathered[9], "dp", axis=0, tiled=True),
        lax.all_gather(gathered[10], "dp", axis=0, tiled=True),
        lax.all_gather(gathered[11], "dp", axis=0, tiled=True),
    )
    hidden_both = row_sets[0]
    upstream_low = row_sets[1]
    gain_one, shift_one, pair_full, dense_bias, gain_two, shift_two, expand_bias, shrink_bias = [
        vector.astype(wide_type) for vector in row_sets[2:]
    ]
    inputs_both = hidden_both.astype(wide_type)
    normed_low = layer_norm(inputs_both, gain_one, shift_one).astype(half_type)
    pair_heads = lax.dynamic_slice_in_dim(
        pair_full.reshape(head_total, 2, head_dim), dp_index * local_heads, local_heads, 0
    )
    triple_bias = jnp.stack(
        [pair_heads[:, 0], jnp.zeros_like(pair_heads[:, 0]), pair_heads[:, 1]], 0
    )
    projected = jnp.einsum(
        "mstd,dhce->cmshte", normed_low, triple_full, preferred_element_type=wide_type
    )
    projected = projected + triple_bias[:, None, None, :, None, :]
    project_low = projected.astype(half_type).reshape(3, seq_count, pair_local, seq_rows, head_dim)
    pair_rows = lax.all_to_all(project_low, "seq", split_axis=1, concat_axis=3, tiled=True)[:, 0]
    query_all, key_all, value_all = (pair_rows[0], pair_rows[1], pair_rows[2])
    pair_index = seq_index * pair_local + jnp.arange(pair_local, dtype=jnp.int32)
    head_index = dp_index * local_heads + pair_index % local_heads
    sequence_index = pair_index // local_heads
    slopes = jnp.power(jnp.float32(2.0), -8.0 * (head_index.astype(wide_type) + 1.0) / head_total)
    prefix_flat = prefix_lengths.reshape(-1)
    prefix_slots = jnp.arange(prefix_flat.shape[0], dtype=jnp.int32)
    prefixes = jnp.sum(
        jnp.where(prefix_slots[None, :] == sequence_index[:, None], prefix_flat[None, :], 0), 1
    )

    def block_scores(pair_item, first_row):
        query_block = lax.dynamic_slice_in_dim(
            lax.dynamic_index_in_dim(query_all, pair_item, 0, False), first_row, block_rows, 0
        )
        keys_item = lax.dynamic_index_in_dim(key_all, pair_item, 0, False)
        head_slope = lax.dynamic_index_in_dim(slopes, pair_item, 0, False)
        prefix = lax.dynamic_index_in_dim(prefixes, pair_item, 0, False)
        query_pos = first_row + jnp.arange(block_rows, dtype=jnp.int32)
        raw_scores = (
            jnp.einsum("qe,ke->qk", query_block, keys_item, preferred_element_type=wide_type)
            * score_scale
        )
        distance = jnp.abs(query_pos[:, None] - key_pos[None, :]).astype(wide_type)
        raw_scores = raw_scores - head_slope * distance
        allowed = (key_pos[None, :] <= query_pos[:, None]) | (key_pos[None, :] < prefix)
        return (query_block, jnp.where(allowed, raw_scores, jnp.float32(-1e30)))

    def forward_block(flat_index):
        pair_item = flat_index // block_count
        first_row = flat_index % block_count * block_rows
        query_block, scores = block_scores(pair_item, first_row)
        row_max = jnp.max(scores, -1, keepdims=True)
        powers = jnp.exp(scores - row_max)
        row_total = jnp.sum(powers, -1, keepdims=True)
        probs_low = (powers / row_total).astype(half_type)
        values_item = lax.dynamic_index_in_dim(value_all, pair_item, 0, False)
        mixed = jnp.dot(probs_low, values_item, preferred_element_type=wide_type).astype(half_type)
        return (mixed, (row_max + jnp.log(row_total))[:, 0])

    mixed_blocks, log_blocks = lax.map(
        forward_block, jnp.arange(pair_local * block_count, dtype=jnp.int32)
    )
    mixed_pairs = mixed_blocks.reshape(pair_local, seq_count, seq_rows, head_dim)
    log_totals = log_blocks.reshape(pair_local, seq_length)
    mixed_home = lax.all_to_all(mixed_pairs, "seq", split_axis=1, concat_axis=0, tiled=True)
    mixed_tokens = jnp.transpose(
        mixed_home.reshape(micro_count, group_count, local_heads, seq_rows, head_dim),
        (0, 1, 3, 2, 4),
    ).reshape(micro_count, group_count, seq_rows, local_heads * head_dim)
    dense_part = jnp.einsum(
        "mstk,kf->mstf", mixed_tokens, dense_full, preferred_element_type=wide_type
    )
    attention_sum = lax.psum(dense_part.astype(jnp.bfloat16), "dp").astype(jnp.float32)
    middle = inputs_both + attention_sum + dense_bias
    gain_rows_two = jnp.broadcast_to(gain_two[None, :], (group_count, model_width))
    shift_rows_two = jnp.broadcast_to(shift_two[None, :], (group_count, model_width))
    normed_two, norm_two_pull = jax.vjp(split_norm, middle, gain_rows_two, shift_rows_two)
    normed_two_low = normed_two.astype(half_type)
    unit_bias = lax.dynamic_slice_in_dim(expand_bias, dp_index * unit_local, unit_local, 0)
    hidden_pre = (
        jnp.einsum("mstd,df->mstf", normed_two_low, expand_full, preferred_element_type=wide_type)
        + unit_bias
    )
    activated_value, gelu_pull = jax.vjp(gelu_tanh, hidden_pre)
    activated_low = activated_value.astype(half_type)
    feed_part = jnp.einsum(
        "mstf,fd->mstd", activated_low, shrink_full, preferred_element_type=wide_type
    )
    feed_sum = lax.psum_scatter(
        feed_part.astype(jnp.bfloat16), "dp", scatter_dimension=1, tiled=True
    ).astype(jnp.float32)
    middle_own = lax.dynamic_slice_in_dim(middle, dp_index, 1, 1)
    layer_output = (middle_own + feed_sum + shrink_bias).astype(half_type)
    triple_back, dense_back, expand_back, shrink_back = (
        lax.all_gather(triple_weight, "seq", axis=0, tiled=True),
        lax.all_gather(dense_weight, "seq", axis=0, tiled=True),
        lax.all_gather(expand_weight, "seq", axis=0, tiled=True),
        lax.all_gather(shrink_weight, "seq", axis=0, tiled=True),
    )
    grad_act = jnp.einsum(
        "mstd,fd->mstf", upstream_low, shrink_back, preferred_element_type=wide_type
    )
    grad_pre_low = gelu_pull(grad_act)[0].astype(half_type)
    norm_two_part = jnp.einsum(
        "mstf,df->mstd", grad_pre_low, expand_back, preferred_element_type=wide_type
    )
    grad_normed_two = lax.psum(norm_two_part.astype(jnp.bfloat16), "dp").astype(jnp.float32)
    grad_middle_norm, grad_gain_rows_two, grad_shift_rows_two = norm_two_pull(grad_normed_two)
    grad_middle = upstream_low.astype(wide_type) + grad_middle_norm
    grad_branch_low = grad_middle.astype(half_type)
    go_pairs = jnp.einsum(
        "mstf,hef->mshte",
        grad_branch_low,
        dense_back.reshape(local_heads, head_dim, model_width),
        preferred_element_type=wide_type,
    ).astype(half_type)
    go_pairs = go_pairs.reshape(seq_count, pair_local, seq_rows, head_dim)
    grad_mixed_pairs = lax.all_to_all(go_pairs, "seq", split_axis=0, concat_axis=2, tiled=True)[0]

    def backward_item(pair_item):
        keys_item = lax.dynamic_index_in_dim(key_all, pair_item, 0, False)
        values_item = lax.dynamic_index_in_dim(value_all, pair_item, 0, False)
        grad_mixed_item = lax.dynamic_index_in_dim(grad_mixed_pairs, pair_item, 0, False)
        totals_item = lax.dynamic_index_in_dim(log_totals, pair_item, 0, False)

        def backward_block(running, block_index):
            key_grad, value_grad = running
            first_row = block_index * block_rows
            query_block, scores = block_scores(pair_item, first_row)
            soft_probs = jnp.exp(
                scores - lax.dynamic_slice_in_dim(totals_item, first_row, block_rows, 0)[:, None]
            )
            grad_block = lax.dynamic_slice_in_dim(grad_mixed_item, first_row, block_rows, 0)
            grad_probs = jnp.einsum(
                "qe,ke->qk", grad_block, values_item, preferred_element_type=wide_type
            )
            row_inner = jnp.sum(grad_probs * soft_probs, -1, keepdims=True)
            grad_scores_low = (soft_probs * (grad_probs - row_inner)).astype(half_type)
            query_grad = (
                jnp.dot(grad_scores_low, keys_item, preferred_element_type=wide_type) * score_scale
            )
            key_grad = (
                key_grad
                + jnp.einsum(
                    "qk,qe->ke", grad_scores_low, query_block, preferred_element_type=wide_type
                )
                * score_scale
            )
            value_grad = value_grad + jnp.einsum(
                "qk,qe->ke",
                soft_probs.astype(half_type),
                grad_block,
                preferred_element_type=wide_type,
            )
            return ((key_grad, value_grad), query_grad)

        zero_rows = jnp.zeros((seq_length, head_dim), wide_type)
        (key_grad, value_grad), query_grads = lax.scan(
            backward_block, (zero_rows, zero_rows), jnp.arange(block_count, dtype=jnp.int32)
        )
        return jnp.stack(
            [query_grads.reshape(seq_length, head_dim), key_grad, value_grad], 0
        ).astype(half_type)

    grad_pairs = lax.map(backward_item, jnp.arange(pair_local, dtype=jnp.int32))
    grad_split = grad_pairs.reshape(pair_local, 3, seq_count, seq_rows, head_dim)
    grad_home = lax.all_to_all(grad_split, "seq", split_axis=2, concat_axis=0, tiled=True)
    grad_project_low = jnp.transpose(
        grad_home.reshape(micro_count, group_count, local_heads, 3, seq_rows, head_dim),
        (0, 1, 4, 2, 3, 5),
    ).reshape(micro_count, group_count, seq_rows, project_width)
    norm_one_part = jnp.einsum(
        "mstc,dc->mstd",
        grad_project_low,
        triple_back.reshape(model_width, project_width),
        preferred_element_type=wide_type,
    )
    grad_normed_one = lax.psum_scatter(
        norm_one_part.astype(jnp.bfloat16), "dp", scatter_dimension=1, tiled=True
    ).astype(jnp.float32)
    inputs_own = hidden.astype(wide_type)
    grad_inputs_norm, grad_gain_one, grad_shift_one = jax.vjp(
        layer_norm, inputs_own, gain_one, shift_one
    )[1](grad_normed_one)
    grad_middle_own = lax.dynamic_slice_in_dim(grad_middle, dp_index, 1, 1)
    hidden_grad = (grad_middle_own + grad_inputs_norm).astype(half_type)
    head_sums = jnp.sum(
        grad_project_low.reshape(micro_count, group_count, seq_rows, local_heads, 3, head_dim),
        (0, 1, 2),
        dtype=wide_type,
    )
    pair_grad = place_half(jnp.stack([head_sums[:, 0], head_sums[:, 2]], 1), dp_index, group_count)
    unit_grad = place_half(jnp.sum(grad_pre_low, (0, 1, 2), dtype=wide_type), dp_index, group_count)
    dense_shift_term = jnp.sum(
        lax.dynamic_slice_in_dim(grad_branch_low, dp_index, 1, 1), (0, 1, 2), dtype=wide_type
    )
    shrink_shift_term = jnp.sum(cotangent, (0, 1, 2), dtype=wide_type)
    gain_two_term = lax.dynamic_index_in_dim(grad_gain_rows_two, dp_index, 0, False)
    shift_two_term = lax.dynamic_index_in_dim(grad_shift_rows_two, dp_index, 0, False)
    vector_sums = (
        lax.psum_scatter(grad_gain_one, ("dp", "seq"), scatter_dimension=0, tiled=True),
        lax.psum_scatter(grad_shift_one, ("dp", "seq"), scatter_dimension=0, tiled=True),
        lax.psum_scatter(pair_grad, ("dp", "seq"), scatter_dimension=0, tiled=True),
        lax.psum_scatter(dense_shift_term, ("dp", "seq"), scatter_dimension=0, tiled=True),
        lax.psum_scatter(gain_two_term, ("dp", "seq"), scatter_dimension=0, tiled=True),
        lax.psum_scatter(shift_two_term, ("dp", "seq"), scatter_dimension=0, tiled=True),
        lax.psum_scatter(unit_grad, ("dp", "seq"), scatter_dimension=0, tiled=True),
        lax.psum_scatter(shrink_shift_term, ("dp", "seq"), scatter_dimension=0, tiled=True),
    )
    normed_flat = normed_low.reshape(token_total, model_width)
    project_flat = grad_project_low.reshape(token_total, project_width)
    normed_two_flat = normed_two_low.reshape(token_total, model_width)
    pre_flat = grad_pre_low.reshape(token_total, unit_local)
    column_sums = lax.psum_scatter(
        jnp.concatenate(
            [
                jnp.einsum(
                    "tr,tc->rc", normed_flat, project_flat, preferred_element_type=wide_type
                ),
                jnp.einsum(
                    "tr,tc->rc", normed_two_flat, pre_flat, preferred_element_type=wide_type
                ),
            ],
            1,
        ),
        "seq",
        scatter_dimension=0,
        tiled=True,
    )
    triple_grad = column_sums[:, :project_width].reshape(
        model_width // seq_count, local_heads, 3, head_dim
    )
    expand_grad = column_sums[:, project_width:]
    dense_rows = dense_weight.shape[0]
    shrink_rows = shrink_weight.shape[0]
    row_block = dense_rows + shrink_rows
    mixed_flat = mixed_tokens.reshape(token_total, local_heads * head_dim)
    branch_flat = grad_branch_low.reshape(token_total, model_width)
    active_flat = activated_low.reshape(token_total, unit_local)
    upstream_flat = upstream_low.reshape(token_total, model_width)
    block_number = row_block * lax.axis_size("seq") // row_block
    dense_term = jnp.einsum("tr,td->rd", mixed_flat, branch_flat, preferred_element_type=wide_type)
    shrink_term = jnp.einsum(
        "tr,td->rd", active_flat, upstream_flat, preferred_element_type=wide_type
    )
    row_sums = lax.psum_scatter(
        jnp.concatenate(
            [
                dense_term.reshape(block_number, dense_rows, model_width),
                shrink_term.reshape(block_number, shrink_rows, model_width),
            ],
            1,
        ).reshape(row_block * lax.axis_size("seq"), model_width),
        "seq",
        scatter_dimension=0,
        tiled=True,
    )
    dense_grad = row_sums[:dense_rows]
    shrink_grad = row_sums[dense_rows:]
    return (
        layer_output,
        hidden_grad,
        vector_sums[0],
        vector_sums[1],
        triple_grad,
        vector_sums[2],
        dense_grad,
        vector_sums[3],
        vector_sums[4],
        vector_sums[5],
        expand_grad,
        vector_sums[6],
        shrink_grad,
        vector_sums[7],
    )


def solution(mesh):
    placed = (
        P(None, "dp", "seq", None),
        P(),
        P(None, "dp", "seq", None),
        P(("dp", "seq")),
        P(("dp", "seq")),
        P("seq", "dp", None, None),
        P(("dp", "seq")),
        P(("dp", "seq"), None),
        P(("dp", "seq")),
        P(("dp", "seq")),
        P(("dp", "seq")),
        P("seq", "dp"),
        P(("dp", "seq")),
        P(("dp", "seq"), None),
        P(("dp", "seq")),
    )
    return jax.shard_map(
        shards,
        mesh=mesh,
        in_specs=placed,
        out_specs=(
            P(None, "dp", "seq", None),
            P(None, "dp", "seq", None),
            P(("dp", "seq")),
            P(("dp", "seq")),
            P("seq", "dp", None, None),
            P(("dp", "seq")),
            P(("dp", "seq"), None),
            P(("dp", "seq")),
            P(("dp", "seq")),
            P(("dp", "seq")),
            P("seq", "dp"),
            P(("dp", "seq")),
            P(("dp", "seq"), None),
            P(("dp", "seq")),
        ),
        check_vma=False,
    )
```

profile of v0, /device:TPU:10, one launch (start us, length us, event | category | flops | bytes accessed | tf_op | source)
XLA Modules:
  0.0 3429.9 jit_solution(780604584698567036)
XLA Ops:
  10.2 30.3 all-gather
  49.4 78.1 %all-reduce.17 = (bf16[1024]{0:T(1024)(128)(2,1)S(1)}, bf16[1024]{0:T(1024)(128)(2,1)S(1)}, bf16[1024]{0:T(1024)(128)(2,1)S(1)}, bf16[1024]{0:T(1024)(128)(2,1)S...) all-reduce(bf16[1024]{0:T(1024)(128)(2,1)S(1)} %dynamic-update-slic, ...), channel_id=1, replica_groups=mesh['dp'=2,'seq'=16] {'seq'}, use_global_device_ids=true, to_apply=%add.1 | all-reduce | flops 6144 | bytes 24576
  137.8 39.5 %all-gather.11.cloned.1.call-done = bf16[2048,8,3,128]{3,0,2,1:T(8,128)(2,1)} async-done(((bf16[128,8,3,128]{3,0,2,1:T(8,128)(2,1)}), bf16[2048,8,3,128]{3,0,2,1:T(8,128)(2,1)}) %all-gather.11.cloned.1.call-update) | async-done | bytes 12582928 | tf_op jit(solution)/shard_map/all_gather | solution.py:72
  177.3 12.9 fusion.55
  190.2 6.8 all-to-all-start
  198.2 95.9 %all-to-all-done = bf16[3,16,4,64,128]{4,3,0,2,1:T(8,128)(2,1)} async-done(((bf16[3,16,4,64,128]{4,3,0,2,1:T(8,128)(2,1)}), bf16[3,16,4,64,128]{4,3,0,2,1:T(8,128)(2,1)}, u32[]{:S(2)}, u32[]{:S(2)}) %all-to-all-start) | async-done | bytes 3145760 | tf_op jit(solution)/shard_map/all_to_all | solution.py:121
  299.8 81.1 %while.69 = (s32[]{:T(128)}, bf16[8,512,128]{2,1,0:T(8,128)(2,1)S(1)}, f32[8,512]{1,0:T(8,128)S(1)}, s32[8]{0:T(128)S(1)}, s32[4]{0:T(128)S(1)}, /*index=5*/bf16...) while((s32[]{:T(128)}, ...), condition=%wide.region_6.7_spmd.clone.clone, body=%wide.region_3.6_spmd.clone.clone.sunk | while | flops 276366368 | bytes 7105556 | solution.py:162
  304.8 2.9 fusion.153
  314.9 2.9 fusion.153
  325.1 2.9 fusion.153
  335.2 2.9 fusion.153
  345.3 2.9 fusion.153
  355.5 2.9 fusion.153
  365.6 2.9 fusion.153
  375.8 2.9 fusion.153
  381.9 9.5 all-to-all-start.1
  391.7 19.6 all-to-all-done.1
  411.3 6.2 fusion.77
  421.3 30.2 all-gather.1
  462.1 169.5 %all-gather.15.cloned.1.call-done = bf16[2048,4096]{1,0:T(8,128)(2,1)} async-done(((bf16[128,4096]{1,0:T(8,128)(2,1)}), bf16[2048,4096]{1,0:T(8,128)(2,1)}) %all-gather.15.cloned.1.call-update) | async-done | bytes 16777232 | tf_op jit(solution)/shard_map/all_gather | solution.py:74
  631.6 18.1 multiply_convert_fusion.1
  649.6 187.1 %all-gather.17.cloned.1.call-done = bf16[4096,2048]{1,0:T(8,128)(2,1)} async-done(((bf16[256,2048]{1,0:T(8,128)(2,1)}), bf16[4096,2048]{1,0:T(8,128)(2,1)}) %all-gather.17.cloned.1.call-update) | async-done | bytes 16777232 | tf_op jit(solution)/shard_map/all_gather | solution.py:75
  836.7 22.4 convert_reduce_fusion
  859.1 15.0 fusion.74
  874.1 21.8 all-reduce.26.cloned.1.call-done
  895.9 4.9 convert_reduce_fusion.2
  903.3 3.2 fusion.109
  906.5 3.3 fusion.96
  909.9 7.2 all-to-all-start.2
  917.1 25.0 all-to-all-done.2
  943.2 151.1 %while.71 = (s32[]{:T(128)}, bf16[4,3,1024,128]{3,2,1,0:T(8,128)(2,1)}, s32[4]{0:T(128)S(1)}, f32[4,1024]{1,0:T(4,128)S(1)}, bf16[4,1024,128]{2,1,0:T(8,128)(2,1...) while((s32[]{:T(128)}, ...), condition=%wide.region_18.19_spmd.clone.clone, body=%wide.region_14.18_spmd.clone.clone.sunk | while | flops 682820608 | bytes 27826516 | solution.py:267
  952.0 24.9 while.72
  954.0 2.9 subtract_exponential_fusion.3
  989.8 24.9 while.72
  991.8 2.9 subtract_exponential_fusion.3
  1004.0 2.9 subtract_exponential_fusion.3
  1027.6 24.9 while.72
  1029.5 2.9 subtract_exponential_fusion.3
  1041.8 2.9 subtract_exponential_fusion.3
  1065.3 24.9 while.72
  1067.3 2.9 subtract_exponential_fusion.3
  1094.3 4.5 copy.98
  1098.8 6.2 all-to-all-start.3
  1114.5 14.5 fusion.71
  1129.1 43.0 %all-to-all-done.3 = bf16[4,3,16,64,128]{4,3,1,0,2:T(8,128)(2,1)S(1)} async-done(((bf16[4,3,16,64,128]{4,3,1,0,2:T(8,128)(2,1)}), bf16[4,3,16,64,128]{4,3,1,0,2:T(8,128)(2,1)S(1)}, u32[]{:S(2)}, u32[]{:S(2)}) %all-to-all-start.3) | async-done | bytes 3145760 | tf_op jit(solution)/shard_map/all_to_all | solution.py:269
  1172.1 10.7 bitcast_convert_fusion
  1184.2 6.6 copy.103
  1190.8 20.3 fusion.118
  1212.5 5.5 fusion.117
  1219.4 2.9 fusion.89
  1222.3 3.8 fusion.91
  1226.2 27.8 pad_maximum_fusion.1
  1254.7 18.6 convolution_bitcast_fusion
  1273.3 4.6 copy.99
  1278.0 7.6 reshape_reshape.6
  1285.6 13.5 fusion.116
  1299.1 38.7 %pad_maximum_fusion = f32[2048,7168]{1,0:T(8,128)} fusion(f32[2048,4096]{1,0:T(8,128)} %convolution_bitcast_fusion, f32[2048,3072]{1,0:T(8,128)} %fusion.116), kind=kLoop, calls=%fused_computation.58 | loop fusion | flops 14680064 | bytes 117440512 | tf_op jit(solution)/shard_map/concatenate | solution.py:317
  1340.7 3.8 add_convert_fusion.2
  1344.5 4.0 add_convert_fusion.1
  1348.5 7.5 all-reduce.28.cloned.1.call-done
  1366.2 850.1 %reduce-scatter.11.cloned.1.call-done = f32[320,2048]{1,0:T(8,128)} async-done(((f32[5120,2048]{1,0:T(8,128)}), f32[320,2048]{1,0:T(8,128)}) %reduce-scatter.11.cloned.1.call-update) | async-done | bytes 2621456 | tf_op jit(solution)/shard_map/reduce_scatter | solution.py:348
  2218.1 3.1 slice.57
  2221.3 1194.7 %reduce-scatter.9.cloned.1.call-done = f32[128,7168]{1,0:T(8,128)} async-done(((f32[2048,7168]{1,0:T(8,128)}), f32[128,7168]{1,0:T(8,128)}) %reduce-scatter.9.cloned.1.call-update) | async-done | bytes 3670032 | tf_op jit(solution)/shard_map/reduce_scatter | solution.py:316
  3419.4 3.1 slice.56
  (440 shorter events, 236.8 us)
Async XLA Ops:
  7.2 124.0 %all-gather.9.cloned.1.call-start = ((), (), s32[]{:S(2)}) async-start(), calls=%async_computation.6 | async-start | bytes 3145728 | tf_op jit(solution)/shard_map/all_gather | solution.py:92
  7.9 169.4 %all-gather.11.cloned.1.call-start = ((), (), s32[]{:S(2)}) async-start(), calls=%async_computation.7 | async-start | bytes 13369344 | tf_op jit(solution)/shard_map/all_gather | solution.py:72
  131.2 6.6 copy-start.14
  131.2 4.4 copy-start.3
  190.2 7.5 copy-start.28
  190.2 103.8 %all-to-all-start = ((bf16[3,16,4,64,128]{4,3,0,2,1:T(8,128)(2,1)}), bf16[3,16,4,64,128]{4,3,0,2,1:T(8,128)(2,1)}, u32[]{:S(2)}, u32[]{:S(2)}) async-start(bf16[3,16,4,64,128]{4,3,0,2,1:T(8,128)(2,1)} %bitcast.292), calls=%async_computation | async-start | bytes 6291456 | tf_op jit(solution)/shard_map/all_to_all | solution.py:121
  197.0 194.6 %all-gather.13.cloned.1.call-start = ((), (), s32[]{:S(2)}) async-start(), calls=%async_computation.8 | async-start | bytes 4456448 | tf_op jit(solution)/shard_map/all_gather | solution.py:73
  381.9 29.3 all-to-all-start.1
  391.4 65.7 %all-reduce.24.cloned.1.call-start = ((), (), s32[]{:S(2)}) async-start(), calls=%async_computation.9 | async-start | bytes 4194304 | tf_op jit(solution)/shard_map/psum | solution.py:175
  411.3 6.2 copy-start.11
  417.5 3.8 copy-start.30
  417.5 214.0 %all-gather.15.cloned.1.call-start = ((), (), s32[]{:S(2)}) async-start(), calls=%async_computation.10 | async-start | bytes 17825792 | tf_op jit(solution)/shard_map/all_gather | solution.py:74
  418.1 231.5 %all-gather.19.cloned.1.call-start = ((), (), s32[]{:S(2)}) async-start(), calls=%async_computation.12 | async-start | bytes 3145728 | tf_op jit(solution)/shard_map/all_gather | solution.py:93
  418.7 418.0 %all-gather.17.cloned.1.call-start = ((), (), s32[]{:S(2)}) async-start(), calls=%async_computation.11 | async-start | bytes 17825792 | tf_op jit(solution)/shard_map/all_gather | solution.py:75
  419.4 476.5 %all-reduce.26.cloned.1.call-start = ((), (), s32[]{:S(2)}) async-start(), calls=%async_computation.13 | async-start | bytes 4194304 | tf_op jit(solution)/shard_map/psum | solution.py:209
  453.4 178.1 %copy-start.25 = (f32[2048]{0:T(1024)}, f32[2048]{0:T(1024)S(1)}, u32[]{:S(2)}) copy-start(f32[2048]{0:T(1024)S(1)} %convert_element_type.169) | copy-start | bytes 24580
  455.3 448.0 %copy-start.16 = (f32[2048]{0:T(1024)}, f32[2048]{0:T(1024)S(1)}, u32[]{:S(2)}) copy-start(f32[2048]{0:T(1024)S(1)} %convert_element_type.168) | copy-start | bytes 24580
  459.5 2.0 copy-start.1
  459.5 443.8 %copy-start.18 = (f32[4,2,64]{2,1,0:T(2,128)}, f32[4,2,64]{2,1,0:T(2,128)S(1)}, u32[]{:S(2)}) copy-start(f32[4,2,64]{2,1,0:T(2,128)S(1)} %broadcast_multiply_fusion) | copy-start | bytes 6148
  462.0 441.3 %copy-start.22 = (f32[4,2,64]{2,1,0:T(2,128)}, f32[4,2,64]{2,1,0:T(2,128)S(1)}, u32[]{:S(2)}) copy-start(f32[4,2,64]{2,1,0:T(2,128)S(1)} %fusion.102) | copy-start | bytes 6148
  895.9 4.9 copy-start.2
  895.9 4.9 copy-start.5
  900.8 2.5 copy-start.12
  903.3 3.2 copy-start.29
  906.5 3.3 copy-start.9
  909.9 32.2 all-to-all-start.2
  958.6 4.4 copy-start
  958.6 4.4 copy-start.6
  963.5 0.7 copy-start.7
  970.8 4.9 copy-start
  970.8 4.8 copy-start.6
  976.2 0.7 copy-start.7
  996.4 4.4 copy-start
  996.4 4.4 copy-start.6
  1001.3 0.7 copy-start.7
  1008.6 4.9 copy-start
  1008.6 4.8 copy-start.6
  1014.0 0.7 copy-start.7
  1034.1 4.4 copy-start
  1034.2 4.4 copy-start.6
  1039.1 0.7 copy-start.7
  1046.4 4.9 copy-start
  1046.4 4.8 copy-start.6
  1051.7 0.7 copy-start.7
  1071.9 4.4 copy-start
  1071.9 4.4 copy-start.6
  1084.2 4.9 copy-start
  1084.2 4.8 copy-start.6
  1098.8 6.3 copy-start.31
  1098.8 73.2 %all-to-all-start.3 = ((bf16[4,3,16,64,128]{4,3,1,0,2:T(8,128)(2,1)}), bf16[4,3,16,64,128]{4,3,1,0,2:T(8,128)(2,1)S(1)}, u32[]{:S(2)}, u32[]{:S(2)}) async-start(bf16[4,3,16,64,128]{4,3,1,0,2:T(8,128)(2,1)} %copy.98), calls=%async_computation.3 | async-start | bytes 6291456 | tf_op jit(solution)/shard_map/all_to_all | solution.py:269
  1105.0 114.4 %all-reduce.30.cloned.1.call-start = ((), (), s32[]{:S(2)}) async-start(), calls=%async_computation.17 | async-start | bytes 8388608
  1182.8 0.7 copy-start.24
  1182.8 173.2 %all-reduce.28.cloned.1.call-start = ((), (), s32[]{:S(2)}) async-start(), calls=%async_computation.16 | async-start | bytes 196608
  1190.8 20.3 copy-start.10
  1190.8 21.1 copy-start.20
  1190.8 21.1 copy-start.21
  1190.8 21.7 copy-start.13
  1212.5 6.9 copy-start.15
  1226.2 990.1 %reduce-scatter.11.cloned.1.call-start = ((), (), s32[]{:S(2)}) async-start(), calls=%async_computation.15 | async-start | bytes 44564480 | tf_op jit(solution)/shard_map/reduce_scatter | solution.py:348
  1254.0 0.7 copy-start.26
  1254.0 2161.9 %reduce-scatter.9.cloned.1.call-start = ((), (), s32[]{:S(2)}) async-start(), calls=%async_computation.14 | async-start | bytes 62390272 | tf_op jit(solution)/shard_map/reduce_scatter | solution.py:316
  1337.8 6.7 copy-start.4
  1337.8 6.7 copy-start.8
  3416.0 1.4 slice-start
  (6 other events, 4.2 us)
Sparse Core Ops, SparseCore 0:
  9.5 11.9 all-gather.8
  24.9 152.3 all-gather.10
  200.6 106.9 all-gather.12
  417.6 21.1 all-reduce.23
  441.5 190.0 all-gather.14
  632.9 10.8 all-gather.18
  646.6 190.0 all-gather.16
  874.2 21.6 all-reduce.25
  1182.9 29.9 all-reduce.29
  1226.3 129.6 all-reduce.27
  1358.4 857.8 reduce-scatter.10
  2218.5 1197.4 reduce-scatter.8
where the time goes:
time: 3440 us; the launch traced here: 3430 us
  waiting for transfers between devices  2660 us (77%)
  matrix products  272 us (8%)
  blocking collectives  154 us (4%)
  other arithmetic  139 us (4%)
  local copies, waits for them, and re-layouts  127 us (4%)
  loops' own time  34.9 us (1%)
    reduce_scatter x1, waiting for transfers between devices, shards(): lax.psum_scatter(jnp.concatenate([jnp.einsum('tr,tc->rc', normed_flat, pr...  1190 us
    reduce_scatter x1, waiting for transfers between devices, shards(): lax.psum_scatter(jnp.concatenate([dense_term.reshape(block_number, dense_...  850 us
    all_gather x1, waiting for transfers between devices, shards(): lax.all_gather(shrink_weight, 'seq', axis=0, tiled=True)  187 us
    all_gather x1, waiting for transfers between devices, shards(): lax.all_gather(expand_weight, 'seq', axis=0, tiled=True)  169 us
    all_to_all x1, waiting for transfers between devices, shards(): lax.all_to_all(project_low, 'seq', split_axis=1, concat_axis=3, tiled=True)  95.9 us
    unnamed x1, blocking collectives  78.1 us
  transfers between devices with their start and end apart: 16, of which 11 were waited for; matrix products, arithmetic and copies ran while one was open for 9% of the time, Pallas kernels for 0%

commit v1 on v0

--- a/solution.py
+++ b/solution.py
@@ -3,6 +3,7 @@
 import jax
 import jax.numpy as jnp
 from jax import lax
+from jax.sharding import Mesh
 from jax.sharding import PartitionSpec as P
 
 EPSILON = 1e-05
@@ -377,43 +378,397 @@
     )
 
 
+def spread_rows(rows):
+    return lax.all_to_all(rows, "z", split_axis=0, concat_axis=0, tiled=True)
+
+
+def gather_columns(blocks):
+    turned = lax.all_to_all(blocks, ("y", "x"), split_axis=0, concat_axis=0, tiled=True)
+    return lax.all_gather(
+        turned.reshape(-1, turned.shape[2]), "z", axis=0, tiled=True
+    )
+
+
+def scatter_columns(term, plane):
+    own = lax.psum_scatter(term, "z", scatter_dimension=0, tiled=True)
+    blocks = own.reshape(plane, own.shape[0] // plane, own.shape[1])
+    return lax.all_to_all(blocks, ("y", "x"), split_axis=0, concat_axis=0, tiled=True)
+
+
+def token_positions(index, rows_y, rows_x, depth, seq_rows):
+    own_rows = depth * seq_rows
+    chip = index // own_rows
+    block = index % own_rows // seq_rows
+    return (block * (rows_y * rows_x) + chip) * seq_rows + index % seq_rows
+
+
+def attend_forward(
+    projected, slopes, prefixes, cores, own_heads, head_dim, rows_y, rows_x, depth, seq_rows
+):
+    wide = jnp.float32
+    length = projected.shape[0] // cores
+    scale = 1.0 / math.sqrt(head_dim)
+    grouped = projected.reshape(cores, length, own_heads, 3, head_dim)
+    pos = token_positions(
+        jnp.arange(length, dtype=jnp.int32), rows_y, rows_x, depth, seq_rows
+    )
+
+    def one(pair):
+        seq, head = pair // own_heads, pair % own_heads
+        item = grouped[seq, :, head]
+        scores = jnp.einsum("qe,ke->qk", item[:, 0], item[:, 1], preferred_element_type=wide)
+        distance = jnp.abs(pos[:, None] - pos[None, :]).astype(wide)
+        scores = scores * scale - slopes[head] * distance
+        allowed = (pos[None, :] <= pos[:, None]) | (pos[None, :] < prefixes[seq])
+        scores = jnp.where(allowed, scores, jnp.float32(-1e30))
+        row_max = jnp.max(scores, -1, keepdims=True)
+        powers = jnp.exp(scores - row_max)
+        total = jnp.sum(powers, -1, keepdims=True)
+        probs = (powers / total).astype(jnp.bfloat16)
+        mixed = jnp.dot(probs, item[:, 2], preferred_element_type=wide).astype(jnp.bfloat16)
+        return mixed, (row_max + jnp.log(total))[:, 0]
+
+    mixed, totals = lax.map(one, jnp.arange(cores * own_heads, dtype=jnp.int32))
+    mixed = mixed.reshape(cores, own_heads, length, head_dim).transpose(0, 2, 1, 3)
+    return mixed.reshape(cores * length, own_heads * head_dim), totals
+
+
+def attend_backward(
+    projected,
+    grad_mixed,
+    totals,
+    slopes,
+    prefixes,
+    cores,
+    own_heads,
+    head_dim,
+    rows_y,
+    rows_x,
+    depth,
+    seq_rows,
+):
+    wide = jnp.float32
+    half = jnp.bfloat16
+    length = projected.shape[0] // cores
+    scale = 1.0 / math.sqrt(head_dim)
+    grouped = projected.reshape(cores, length, own_heads, 3, head_dim)
+    upstream = grad_mixed.reshape(cores, length, own_heads, head_dim)
+    pos = token_positions(
+        jnp.arange(length, dtype=jnp.int32), rows_y, rows_x, depth, seq_rows
+    )
+
+    def one(pair):
+        seq, head = pair // own_heads, pair % own_heads
+        item = grouped[seq, :, head]
+        grad = upstream[seq, :, head]
+        scores = jnp.einsum("qe,ke->qk", item[:, 0], item[:, 1], preferred_element_type=wide)
+        distance = jnp.abs(pos[:, None] - pos[None, :]).astype(wide)
+        scores = scores * scale - slopes[head] * distance
+        allowed = (pos[None, :] <= pos[:, None]) | (pos[None, :] < prefixes[seq])
+        scores = jnp.where(allowed, scores, jnp.float32(-1e30))
+        probs = jnp.exp(scores - totals[pair][:, None])
+        grad_probs = jnp.einsum("qe,ke->qk", grad, item[:, 2], preferred_element_type=wide)
+        inner = jnp.sum(grad_probs * probs, -1, keepdims=True)
+        grad_scores = (probs * (grad_probs - inner)).astype(half)
+        query = jnp.dot(grad_scores, item[:, 1], preferred_element_type=wide) * scale
+        key = jnp.einsum("qk,qe->ke", grad_scores, item[:, 0], preferred_element_type=wide) * scale
+        value = jnp.einsum("qk,qe->ke", probs.astype(half), grad, preferred_element_type=wide)
+        return jnp.stack([query, key, value], 1).astype(half)
+
+    grads = lax.map(one, jnp.arange(cores * own_heads, dtype=jnp.int32))
+    grads = grads.reshape(cores, own_heads, length, 3, head_dim).transpose(0, 2, 1, 3, 4)
+    return grads.reshape(cores * length, own_heads * 3 * head_dim)
+
+
+def planar(
+    hidden,
+    prefix_lengths,
+    cotangent,
+    first_gain,
+    first_shift,
+    triple_weight,
+    pair_bias,
+    dense_weight,
+    dense_shift,
+    second_gain,
+    second_shift,
+    expand_weight,
+    expand_shift,
+    shrink_weight,
+    shrink_shift,
+):
+    wide = jnp.float32
+    half = jnp.bfloat16
+    cores = lax.axis_size("dp")
+    depth = lax.axis_size("z")
+    rows_y = lax.axis_size("y")
+    rows_x = lax.axis_size("x")
+    plane = rows_y * rows_x
+    core = lax.axis_index("dp")
+    at_y = lax.axis_index("y")
+    at_x = lax.axis_index("x")
+    place = at_y * rows_x + at_x
+    seq_rows = hidden.shape[2]
+    width = hidden.shape[3]
+    head_dim = triple_weight.shape[3]
+    heads = triple_weight.shape[1]
+    own_heads = heads // plane
+    length = seq_rows * depth * plane
+    own_rows = seq_rows * depth
+    units = expand_weight.shape[1]
+    own_units = units // plane
+    row_block = expand_weight.shape[0]
+    shrink_rows = shrink_weight.shape[0]
+    group = ("dp", "y", "x")
+
+    pieces = [
+        first_gain,
+        first_shift,
+        dense_shift,
+        second_gain,
+        second_shift,
+        shrink_shift,
+        pair_bias,
+        expand_shift,
+    ]
+    packed = lax.all_gather(
+        jnp.concatenate(pieces), ("dp", "z", "y", "x"), axis=0, tiled=False
+    ).reshape(-1, sum(p.shape[0] for p in pieces))
+    vectors = []
+    offset = 0
+    for piece in pieces:
+        vectors.append(packed[:, offset : offset + piece.shape[0]].reshape(-1).astype(wide))
+        offset += piece.shape[0]
+    gain_one, shift_one, dense_bias, gain_two, shift_two, shrink_bias, pair_full, unit_full = vectors
+    pair_heads = pair_full.reshape(cores, rows_x, own_heads, rows_y, 2, head_dim)[
+        core, at_x, :, at_y
+    ]
+    triple_bias = jnp.stack(
+        [pair_heads[:, 0], jnp.zeros_like(pair_heads[:, 0]), pair_heads[:, 1]], 1
+    ).reshape(-1)
+    unit_bias = unit_full.reshape(cores, depth, plane, shrink_rows)[core, :, place].reshape(-1)
+
+    triple_own = gather_columns(
+        triple_weight.reshape(row_block, rows_x, own_heads, rows_y, 3 * head_dim)
+        .transpose(3, 1, 0, 2, 4)
+        .reshape(plane, row_block, own_heads * 3 * head_dim)
+    )
+    expand_own = gather_columns(
+        expand_weight.reshape(row_block, depth, plane, shrink_rows)
+        .transpose(2, 0, 1, 3)
+        .reshape(plane, row_block, own_units)
+    )
+    shrink_own = lax.all_gather(shrink_weight, "z", axis=0, tiled=True)
+    dense_rows = lax.all_gather(dense_weight, ("z", "x"), axis=0, tiled=True)
+    dense_own = lax.dynamic_slice_in_dim(
+        dense_rows, at_x * own_heads * head_dim, own_heads * head_dim, 0
+    )
+
+    inputs = spread_rows(hidden[:, 0]).reshape(own_rows, width).astype(wide)
+    upstream = spread_rows(cotangent[:, 0]).reshape(own_rows, width)
+
+    def gather_tokens(rows):
+        return lax.all_gather(rows, group, axis=0, tiled=True)
+
+    def scatter_tokens(partial):
+        return lax.psum_scatter(partial, group, scatter_dimension=0, tiled=True).astype(wide)
+
+    normed_own = layer_norm(inputs, gain_one, shift_one).astype(half)
+    normed = gather_tokens(normed_own)
+    upstream_all = gather_tokens(upstream)
+    projected = (
+        jnp.dot(normed, triple_own, preferred_element_type=wide) + triple_bias
+    ).astype(half)
+
+    head_index = core * heads + at_x * own_heads * rows_y + jnp.arange(own_heads) * rows_y + at_y
+    slopes = jnp.power(
+        jnp.float32(2.0), -8.0 * (head_index.astype(wide) + 1.0) / (heads * cores)
+    )
+    at_z = lax.axis_index("z")
+    prefixes = lax.dynamic_index_in_dim(prefix_lengths, at_z, 0, False)
+    mixed, log_totals = attend_forward(
+        projected, slopes, prefixes, cores, own_heads, head_dim, rows_y, rows_x, depth, seq_rows
+    )
+    dense_part = jnp.dot(mixed, dense_own, preferred_element_type=wide).astype(half)
+    middle = inputs + scatter_tokens(dense_part) + dense_bias
+    normed_two_own, norm_two_pull = jax.vjp(layer_norm, middle, gain_two, shift_two)
+    normed_two = gather_tokens(normed_two_own.astype(half))
+    hidden_pre = jnp.dot(normed_two, expand_own, preferred_element_type=wide) + unit_bias
+    activated, gelu_pull = jax.vjp(gelu_tanh, hidden_pre)
+    activated = activated.astype(half)
+    feed_part = jnp.dot(activated, shrink_own, preferred_element_type=wide).astype(half)
+    layer_output = (middle + scatter_tokens(feed_part) + shrink_bias).astype(half)
+    layer_output = spread_rows(layer_output.reshape(depth, seq_rows, width))[:, None]
+
+    grad_act = jnp.einsum("tf,uf->tu", upstream_all, shrink_own, preferred_element_type=wide)
+    grad_pre = gelu_pull(grad_act)[0].astype(half)
+    norm_two_part = jnp.einsum(
+        "tu,du->td", grad_pre, expand_own, preferred_element_type=wide
+    ).astype(half)
+    grad_norm_two, gain_two_term, shift_two_term = norm_two_pull(scatter_tokens(norm_two_part))
+    grad_middle = upstream.astype(wide) + grad_norm_two
+    branch_own = grad_middle.astype(half)
+    branch = gather_tokens(branch_own)
+    shrink_term = jnp.einsum(
+        "tu,td->ud", activated, upstream_all, preferred_element_type=wide
+    ).astype(half)
+    shrink_grad = lax.psum_scatter(shrink_term, "z", scatter_dimension=0, tiled=True).astype(wide)
+    expand_term = jnp.einsum(
+        "td,tu->du", normed_two, grad_pre, preferred_element_type=wide
+    ).astype(half)
+    expand_grad = (
+        scatter_columns(expand_term, plane)
+        .reshape(plane, row_block, depth, shrink_rows)
+        .transpose(1, 2, 0, 3)
+        .reshape(row_block, units)
+        .astype(wide)
+    )
+
+    grad_mixed = jnp.einsum("tf,ef->te", branch, dense_own, preferred_element_type=wide).astype(
+        half
+    )
+    dense_term = jnp.einsum("te,tf->ef", mixed, branch, preferred_element_type=wide).astype(half)
+    dense_wide = lax.dynamic_update_slice_in_dim(
+        jnp.zeros_like(dense_rows), dense_term, at_x * own_heads * head_dim, 0
+    )
+    dense_grad = lax.psum_scatter(
+        dense_wide, ("z", "x"), scatter_dimension=0, tiled=True
+    ).astype(wide)
+    grad_project = attend_backward(
+        projected,
+        grad_mixed,
+        log_totals,
+        slopes,
+        prefixes,
+        cores,
+        own_heads,
+        head_dim,
+        rows_y,
+        rows_x,
+        depth,
+        seq_rows,
+    )
+    norm_one_part = jnp.einsum(
+        "tc,dc->td", grad_project, triple_own, preferred_element_type=wide
+    ).astype(half)
+    grad_norm_one, gain_one_term, shift_one_term = jax.vjp(
+        layer_norm, inputs, gain_one, shift_one
+    )[1](scatter_tokens(norm_one_part))
+    hidden_grad = (grad_middle + grad_norm_one).astype(half)
+    hidden_grad = spread_rows(hidden_grad.reshape(depth, seq_rows, width))[:, None]
+    triple_term = jnp.einsum(
+        "td,tc->dc", normed, grad_project, preferred_element_type=wide
+    ).astype(half)
+    triple_grad = (
+        scatter_columns(triple_term, plane)
+        .reshape(rows_y, rows_x, row_block, own_heads, 3 * head_dim)
+        .transpose(2, 1, 3, 0, 4)
+        .reshape(row_block, heads, 3, head_dim)
+        .astype(wide)
+    )
+
+    head_sums = jnp.sum(grad_project, 0, dtype=wide).reshape(own_heads, 3, head_dim)
+    pair_term = jnp.stack([head_sums[:, 0], head_sums[:, 2]], 1)
+    pair_zero = jnp.zeros((cores, rows_x, own_heads, rows_y, 2, head_dim), wide)
+    pair_wide = lax.dynamic_update_slice(
+        pair_zero, pair_term[None, None, :, None], (core, at_x, 0, at_y, 0, 0)
+    ).reshape(-1)
+    unit_term = jnp.sum(grad_pre, 0, dtype=wide).reshape(1, depth, 1, shrink_rows)
+    unit_wide = lax.dynamic_update_slice(
+        jnp.zeros((cores, depth, plane, shrink_rows), wide), unit_term, (core, 0, place, 0)
+    ).reshape(-1)
+    terms = [
+        gain_one_term,
+        shift_one_term,
+        jnp.sum(branch_own, 0, dtype=wide),
+        gain_two_term,
+        shift_two_term,
+        jnp.sum(upstream, 0, dtype=wide),
+        pair_wide,
+        unit_wide,
+    ]
+    devices = cores * depth * plane
+    summed = lax.psum_scatter(
+        jnp.concatenate([t.reshape(devices, -1) for t in terms], 1),
+        ("dp", "z", "y", "x"),
+        scatter_dimension=0,
+        tiled=True,
+    ).reshape(-1)
+    vector_grads = []
+    offset = 0
+    for piece in pieces:
+        vector_grads.append(summed[offset : offset + piece.shape[0]])
+        offset += piece.shape[0]
+    return (
+        layer_output,
+        hidden_grad,
+        vector_grads[0],
+        vector_grads[1],
+        triple_grad,
+        vector_grads[6],
+        dense_grad,
+        vector_grads[2],
+        vector_grads[3],
+        vector_grads[4],
+        expand_grad,
+        vector_grads[7],
+        shrink_grad,
+        vector_grads[5],
+    )
+
+
 def solution(mesh):
+    depth = 4
+    sides = (2, 2)
+    planar_plan = mesh.shape["seq"] == depth * sides[0] * sides[1]
+    if planar_plan:
+        grid = Mesh(
+            mesh.devices.reshape(mesh.shape["dp"], depth, *sides), ("dp", "z", "y", "x")
+        )
+        seq = ("z", "y", "x")
+    else:
+        grid = mesh
+        seq = ("seq",)
+    tokens = P(None, "dp", seq, None)
+    vector = P(("dp",) + seq)
+    matrix = P(("dp",) + seq, None)
     placed = (
-        P(None, "dp", "seq", None),
+        tokens,
         P(),
-        P(None, "dp", "seq", None),
-        P(("dp", "seq")),
-        P(("dp", "seq")),
-        P("seq", "dp", None, None),
-        P(("dp", "seq")),
-        P(("dp", "seq"), None),
-        P(("dp", "seq")),
-        P(("dp", "seq")),
-        P(("dp", "seq")),
-        P("seq", "dp"),
-        P(("dp", "seq")),
-        P(("dp", "seq"), None),
-        P(("dp", "seq")),
+        tokens,
+        vector,
+        vector,
+        P(seq, "dp", None, None),
+        vector,
+        matrix,
+        vector,
+        vector,
+        vector,
+        P(seq, "dp"),
+        vector,
+        matrix,
+        vector,
+    )
+    results = (
+        tokens,
+        tokens,
+        vector,
+        vector,
+        P(seq, "dp", None, None),
+        vector,
+        matrix,
+        vector,
+        vector,
+        vector,
+        P(seq, "dp"),
+        vector,
+        matrix,
+        vector,
     )
     return jax.shard_map(
-        shards,
-        mesh=mesh,
+        planar if planar_plan else shards,
+        mesh=grid,
         in_specs=placed,
-        out_specs=(
-            P(None, "dp", "seq", None),
-            P(None, "dp", "seq", None),
-            P(("dp", "seq")),
-            P(("dp", "seq")),
-            P("seq", "dp", None, None),
-            P(("dp", "seq")),
-            P(("dp", "seq"), None),
-            P(("dp", "seq")),
-            P(("dp", "seq")),
-            P(("dp", "seq")),
-            P("seq", "dp"),
-            P(("dp", "seq")),
-            P(("dp", "seq"), None),
-            P(("dp", "seq")),
-        ),
+        out_specs=results,
         check_vma=False,
     )

time: 3440 us -> 1430 us (0.42)
  waiting for transfers between devices: 2660 us -> 828 us
  matrix products: 272 us -> 184 us
  other arithmetic: 139 us -> 52.1 us
  blocking collectives: 154 us -> 210 us
  local copies, waits for them, and re-layouts: 127 us -> 88.7 us
    reduce_scatter x2 -> x8, waiting for transfers between devices: 2040 us -> 382 us  [the longest x4 250 us: scatter_tokens(): lax.psum_scatter(partial, group, scatter_dimension=0, tiled=True)]
    all_to_all x4, waiting for transfers between devices: 183 us -> 6.82 us  [the longest x1 6.81 us: scatter_columns(): lax.all_to_all(blocks, ('y', 'x'), split_axis=0, concat_axis=0, tiled=True)]
    unnamed x14 -> x18, waiting for transfers between devices: 10.7 us -> 126 us
    all_to_all x0 -> x4, blocking collectives: none -> 106 us  [the longest x1 56.2 us: spread_rows(): return lax.all_to_all(rows, 'z', split_axis=0, concat_axis=0, tiled=True)]
    dot_general x68 -> x40, matrix products: 272 us -> 184 us  [the longest x8 22.8 us: one(): jnp.einsum('qe,ke->qk', item[:, 0], item[:, 1], preferred_element_type=wide)]
    all_gather x6 -> x8, waiting for transfers between devices: 396 us -> 314 us  [the longest x4 210 us: gather_tokens(): return lax.all_gather(rows, group, axis=0, tiled=True)]
    unnamed x1 -> x0, blocking collectives: 78.1 us -> none
    concatenate x2 -> x0, other arithmetic: 66.5 us -> none  [the longest x1 38.7 us: shards(): jnp.concatenate([jnp.einsum('tr,tc->rc', normed_flat, project_flat, prefe...]
  transfers between devices with their start and end apart: 16 -> 21, of which waited for: 11 -> 14; matrix products, arithmetic and copies ran while one was open for 9% -> 19% of each run, Pallas kernels for 0% -> 0%
where the time goes in v1:
time: 1430 us
  waiting for transfers between devices  828 us (58%)
  blocking collectives  210 us (15%)
  matrix products  184 us (13%)
  local copies, waits for them, and re-layouts  88.7 us (6%)
  other arithmetic  52.1 us (4%)
  loops' own time  26.6 us (2%)
  starting transfers between devices  21.3 us (1%)
  between operations  14.7 us (1%)
    reduce_scatter x4, waiting for transfers between devices, scatter_tokens(): lax.psum_scatter(partial, group, scatter_dimension=0, tiled=True)  250 us
    all_gather x4, waiting for transfers between devices, gather_tokens(): return lax.all_gather(rows, group, axis=0, tiled=True)  210 us
    unnamed x18, waiting for transfers between devices  126 us
    all_gather x1, blocking collectives, planar(): lax.all_gather(jnp.concatenate(pieces), ('dp', 'z', 'y', 'x'), axis=0, ti...  103 us
    reduce_scatter x1, waiting for transfers between devices, planar(): lax.psum_scatter(shrink_term, 'z', scatter_dimension=0, tiled=True)  76.5 us
    all_gather x1, waiting for transfers between devices, planar(): shrink_own = lax.all_gather(shrink_weight, 'z', axis=0, tiled=True)  65.4 us
    all_to_all x1, blocking collectives, spread_rows(): return lax.all_to_all(rows, 'z', split_axis=0, concat_axis=0, tiled=True)  56.2 us
    reduce_scatter x1, waiting for transfers between devices, planar(): lax.psum_scatter(dense_wide, ('z', 'x'), scatter_dimension=0, tiled=True)  55.1 us
  transfers between devices with their start and end apart: 21, of which 14 were waited for; matrix products, arithmetic and copies ran while one was open for 19% of the time, Pallas kernels for 0%

profile of v1, /device:TPU:10, one launch (start us, length us, event | category | flops | bytes accessed | tf_op | source)
XLA Modules:
  0.0 1425.4 jit_solution(6406022825116796092)
XLA Ops:
  9.0 14.3 %all_to_all.40 = bf16[4,128,768]{1,2,0:T(8,128)(2,1)S(1)} all-to-all(bf16[4,128,768]{1,2,0:T(8,128)(2,1)S(1)} %bitcast.260), channel_id=1, replica_groups=mesh['dp'=2,'z'=4,'y'=2,'x'=2] {'y','x'}, dimensions={0} | all-to-all | bytes 1572864 | tf_op jit(solution)/shard_map/all_to_all | solution.py:386
  24.5 5.3 all-to-all-start
  30.0 103.5 %all-gather.1 = bf16[32,1,768]{2,1,0:T(2,128)(2,1)S(1)} all-gather(bf16[1,1,768]{2,1,0:T(2,128)(2,1)S(1)} %reshape.411), channel_id=2, replica_groups=mesh['dp'=2,'z'=4,'y'=2,'x'=2] {'dp','z','y','x'}, dimensions={0}, use_global_device_ids=true | all-gather | bytes 50688 | tf_op jit(solution)/shard_map/all_gather | solution.py:534
  138.1 54.6 %all-gather.11.cloned.1.call-done = bf16[2048,2048]{1,0:T(8,128)(2,1)} async-done(((bf16[256,2048]{1,0:T(8,128)(2,1)}), bf16[2048,2048]{1,0:T(8,128)(2,1)}) %all-gather.11.cloned.1.call-update) | async-done | bytes 8388624 | tf_op jit(solution)/shard_map/all_gather | solution.py:571
  192.7 11.2 add_convert_fusion
  203.8 9.4 reshape.414
  213.2 4.5 copy.60
  217.8 42.6 %while.30 = (s32[]{:T(128)}, bf16[4,1024,128]{2,1,0:T(8,128)(2,1)S(1)}, f32[4,1024]{1,0:T(4,128)S(1)}, s32[4]{0:T(128)S(1)}, s32[2]{0:T(128)S(1)}, /*index=5*/bf...) while((s32[]{:T(128)}, ...), condition=%wide.region_5.6_spmd.clone.clone, body=%wide.region_2.5_spmd.clone.clone.sunk | while | flops 552806400 | bytes 15260080 | solution.py:431
  224.0 2.7 fusion.148
  234.7 2.7 fusion.148
  245.4 2.7 fusion.148
  256.0 2.7 fusion.148
  261.5 7.2 convolution_convert_fusion.3
  270.7 17.0 %all_to_all.41 = bf16[4,128,1024]{1,2,0:T(8,128)(2,1)S(1)} all-to-all(bf16[4,128,1024]{1,2,0:T(8,128)(2,1)S(1)} %bitcast.253), channel_id=1, replica_groups=mesh['dp'=2,'z'=4,'y'=2,'x'=2] {'y','x'}, dimensions={0} | all-to-all | bytes 2097152 | tf_op jit(solution)/shard_map/all_to_all | solution.py:386
  289.2 51.2 %reduce-scatter.9.cloned.1.call-done = bf16[256,2048]{1,0:T(8,128)(2,1)} async-done(((bf16[2048,2048]{1,0:T(8,128)(2,1)}), bf16[256,2048]{1,0:T(8,128)(2,1)}) %reduce-scatter.9.cloned.1.call-update) | async-done | bytes 1048592 | tf_op jit(solution)/shard_map/reduce_scatter | solution.py:574
  342.2 1.9 multiply_reduce_fusion.1
  346.6 56.2 %all_to_all.42 = bf16[4,64,2048]{2,1,0:T(8,128)(2,1)} all-to-all(bf16[4,64,2048]{2,1,0:T(8,128)(2,1)S(1)} %bitcast.262), channel_id=1, replica_groups=mesh['dp'=2,'z'=4,'y'=2,'x'=2] {'z'}, dimensions={0} | all-to-all | bytes 2097152 | tf_op jit(solution)/shard_map/all_to_all | solution.py:382
  402.9 38.5 %all-gather.19.cloned.1.call-done = bf16[2048,1024]{1,0:T(8,128)(2,1)} async-done(((bf16[512,1024]{1,0:T(8,128)(2,1)}), bf16[2048,1024]{1,0:T(8,128)(2,1)}) %all-gather.19.cloned.1.call-update) | async-done | bytes 4194320 | tf_op jit(solution)/shard_map/all_gather | solution.py:387
  441.4 57.8 %all-gather.17.cloned.1.call-done = bf16[2048,2048]{1,0:T(8,128)(2,1)} async-done(((bf16[256,2048]{1,0:T(8,128)(2,1)}), bf16[2048,2048]{1,0:T(8,128)(2,1)}) %all-gather.17.cloned.1.call-update) | async-done | bytes 8388624 | tf_op jit(solution)/shard_map/all_gather | solution.py:571
  499.2 14.4 %fusion.114 = f32[2048,1024]{1,0:T(8,128)} fusion(bf16[2048,2048]{1,0:T(8,128)(2,1)} %all-gather.17.cloned.1.call-done, bf16[2048,1024]{1,0:T(8,128)(2,1)} %all-gather.19.cloned.1.call-done), kind=kOutput, calls=%fused_computation.213 | convolution fusion | flops 8589934592 | bytes 20971520 | tf_op jit(solution)/shard_map/dot_general | solution.py:596
  513.6 65.4 %all-gather.21.cloned.1.call-done = bf16[1024,2048]{1,0:T(8,128)(2,1)} async-done(((bf16[256,2048]{1,0:T(8,128)(2,1)}), bf16[1024,2048]{1,0:T(8,128)(2,1)}) %all-gather.21.cloned.1.call-update) | async-done | bytes 4194320 | tf_op jit(solution)/shard_map/all_gather | solution.py:561
  579.1 57.1 %all-gather.23.cloned.1.call-done = bf16[2048,2048]{1,0:T(8,128)(2,1)} async-done(((bf16[256,2048]{1,0:T(8,128)(2,1)}), bf16[2048,2048]{1,0:T(8,128)(2,1)}) %all-gather.23.cloned.1.call-update) | async-done | bytes 8388624 | tf_op jit(solution)/shard_map/all_gather | solution.py:571
  636.2 20.6 %convert_reduce_fusion = (f32[1024]{0:T(1024)}, bf16[2048,1024]{1,0:T(8,128)(2,1)S(1)}) fusion(f32[2048,1024]{1,0:T(8,128)} %fusion.114, f32[1024]{0:T(1024)S(1)} %bitcast.274, bf16[2048,2048]{1,0:T(8,128)(2,1)} %all-gather.23.cloned.1.call-done, bf16[1024,2048]{1,0:T(8,128)(2,1)} %all-gather.21.cloned.1.call-done), kind=kOutput, calls=%fused_computation.113 | convolution fusion | flops 8646556672 | bytes 25174016 | tf_op jit(solution)/shard_map/tf,uf->tu/dot_general | solution.py:603
  656.7 2.1 copy-done.34
  658.8 11.4 convolution_convert_fusion.1
  670.2 15.6 %convolution_convert_fusion.2 = bf16[2048,2048]{1,0:T(8,128)(2,1)} fusion(bf16[1024,2048]{1,0:T(8,128)(2,1)} %all-gather.21.cloned.1.call-done, f32[2048,1024]{1,0:T(8,128)} %fusion.114, f32[1024]{0:T(1024)S(1)} %bitcast.275), kind=kOutput, calls=%fused_computation.117 | convolution fusion | flops 8615100416 | bytes 20975616 | tf_op jit(solution)/shard_map/dot_general | solution.py:599
  686.7 55.2 %reduce-scatter.13.cloned.1.call-done = bf16[256,2048]{1,0:T(8,128)(2,1)} async-done(((bf16[2048,2048]{1,0:T(8,128)(2,1)}), bf16[256,2048]{1,0:T(8,128)(2,1)}) %reduce-scatter.13.cloned.1.call-update) | async-done | bytes 1048592 | tf_op jit(solution)/shard_map/reduce_scatter | solution.py:574
  741.8 2.9 fusion.83
  744.8 71.9 %reduce-scatter.11.cloned.1.call-done = bf16[256,2048]{1,0:T(8,128)(2,1)} async-done(((bf16[2048,2048]{1,0:T(8,128)(2,1)}), bf16[256,2048]{1,0:T(8,128)(2,1)}) %reduce-scatter.11.cloned.1.call-update) | async-done | bytes 1048592 | tf_op jit(solution)/shard_map/reduce_scatter | solution.py:574
  816.7 3.6 fusion.110
  821.6 2.0 convert_reduce_fusion.6
  823.7 14.1 convolution_convert_fusion.5
  838.0 40.1 %all-gather.25.cloned.1.call-done = bf16[2048,2048]{1,0:T(8,128)(2,1)} async-done(((bf16[256,2048]{1,0:T(8,128)(2,1)}), bf16[2048,2048]{1,0:T(8,128)(2,1)}) %all-gather.25.cloned.1.call-update) | async-done | bytes 8388624 | tf_op jit(solution)/shard_map/all_gather | solution.py:571
  878.1 6.0 convolution_convert_fusion.8
  886.9 62.4 %while.31 = (s32[]{:T(128)}, bf16[4,1024,3,128]{3,1,2,0:T(8,128)(2,1)}, s32[4]{0:T(128)S(1)}, s32[2]{0:T(128)S(1)}, bf16[2,1024,2,3,128]{4,1,3,2,0:T(8,128)(2,1)...) while((s32[]{:T(128)}, ...), condition=%wide.region_15.16_spmd.clone.clone, body=%wide.region_13.15_spmd.clone.clone.sunk | while | flops 1362044928 | bytes 37259752 | solution.py:478
  894.5 3.0 subtract_exponential_fusion.3
  910.1 3.0 subtract_exponential_fusion.3
  925.7 3.0 subtract_exponential_fusion.3
  941.3 3.0 subtract_exponential_fusion.3
  949.3 8.7 copy.67
  958.0 2.9 copy.76
  962.5 10.4 convolution_convert_fusion.6
  973.0 11.9 convolution_convert_fusion
  984.9 16.6 %convolution_convert_fusion.4 = bf16[1024,2048]{1,0:T(8,128)(2,1)} fusion(bf16[2048,2048]{1,0:T(8,128)(2,1)} %all-gather.23.cloned.1.call-done, f32[2048,1024]{1,0:T(8,128)} %fusion.114, f32[1024]{0:T(1024)S(1)} %bitcast.276), kind=kOutput, calls=%fused_computation.121 | convolution fusion | flops 8613003264 | bytes 20975616 | tf_op jit(solution)/shard_map/tu,td->ud/dot_general | solution.py:612
  1003.3 6.8 fusion.76
  1010.2 18.7 %all_to_all.43 = bf16[4,128,1024]{2,1,0:T(8,128)(2,1)} all-to-all(bf16[4,128,1024]{2,1,0:T(8,128)(2,1)} %bitcast.263), channel_id=1, replica_groups=mesh['dp'=2,'z'=4,'y'=2,'x'=2] {'y','x'}, dimensions={0} | all-to-all | bytes 2097152 | tf_op jit(solution)/shard_map/all_to_all | solution.py:395
  1028.9 5.3 all-to-all-start.3
  1034.2 2.3 copy.68
  1036.5 71.7 %reduce-scatter.15.cloned.1.call-done = bf16[256,2048]{1,0:T(8,128)(2,1)} async-done(((bf16[2048,2048]{1,0:T(8,128)(2,1)}), bf16[256,2048]{1,0:T(8,128)(2,1)}) %reduce-scatter.15.cloned.1.call-update) | async-done | bytes 1048592 | tf_op jit(solution)/shard_map/reduce_scatter | solution.py:574
  1108.2 2.0 convert_reduce_fusion.2
  1110.3 2.3 fusion.84
  1112.6 4.7 all-to-all-start.6
  1117.3 3.6 add_convert_fusion.1
  1120.9 6.8 all-to-all-done.6
  1127.7 5.1 all-to-all-start.5
  1133.2 76.5 %reduce-scatter.23.cloned.1.call-done = bf16[256,2048]{1,0:T(8,128)(2,1)} async-done(((bf16[1024,2048]{1,0:T(8,128)(2,1)}), bf16[256,2048]{1,0:T(8,128)(2,1)}) %reduce-scatter.23.cloned.1.call-update) | async-done | bytes 1048592 | tf_op jit(solution)/shard_map/reduce_scatter | solution.py:615
  1209.7 2.8 convert_element_type.299
  1213.4 2.7 copy.87
  1216.1 3.3 reshape.407
  1219.6 5.2 convert_reduce_fusion.1
  1224.9 55.1 %reduce-scatter.19.cloned.1.call-done = bf16[64,2048]{1,0:T(8,128)(2,1)} async-done(((bf16[512,2048]{1,0:T(8,128)(2,1)}), bf16[64,2048]{1,0:T(8,128)(2,1)}) %reduce-scatter.19.cloned.1.call-update) | async-done | bytes 262160 | tf_op jit(solution)/shard_map/reduce_scatter | solution.py:634
  1285.6 124.4 %all-reduce.3.cloned.1.call-done = f32[32,768]{1,0:T(8,128)} async-done(((f32[32,768]{1,0:T(8,128)}), f32[32,768]{1,0:T(8,128)}) %all-reduce.3.cloned.1.call-update) | async-done | bytes 98320
  1414.1 2.3 copy.113
  1416.4 2.3 copy.114
  (276 shorter events, 92.0 us)
Async XLA Ops:
  7.2 130.7 %copy-start = (s32[4,2]{0,1:T(2,128)S(1)}, s32[4,2]{0,1:T(2,128)}, u32[]{:S(2)}) copy-start(s32[4,2]{0,1:T(2,128)} %param.20) | copy-start | bytes 100
  7.2 130.9 %all-gather.13.cloned.1.call-start = ((), (), s32[]{:S(2)}) async-start(), calls=%async_computation.17 | async-start | bytes 3932160 | tf_op jit(solution)/shard_map/all_gather | solution.py:387
  8.9 21.0 %copy-start.25 = (bf16[64]{0:T(256)(128)(2,1)S(1)}, bf16[64]{0:T(256)(128)(2,1)}, u32[]{:S(2)}) copy-start(bf16[64]{0:T(256)(128)(2,1)} %param.22) | copy-start | bytes 388
  8.9 21.0 %copy-start.26 = (bf16[64]{0:T(256)(128)(2,1)S(1)}, bf16[64]{0:T(256)(128)(2,1)}, u32[]{:S(2)}) copy-start(bf16[64]{0:T(256)(128)(2,1)} %param.23) | copy-start | bytes 388
  8.9 21.0 %copy-start.27 = (bf16[64]{0:T(256)(128)(2,1)S(1)}, bf16[64]{0:T(256)(128)(2,1)}, u32[]{:S(2)}) copy-start(bf16[64]{0:T(256)(128)(2,1)} %param.27) | copy-start | bytes 388
  8.9 20.9 %copy-start.28 = (bf16[64]{0:T(256)(128)(2,1)S(1)}, bf16[64]{0:T(256)(128)(2,1)}, u32[]{:S(2)}) copy-start(bf16[64]{0:T(256)(128)(2,1)} %param.28) | copy-start | bytes 388
  8.9 20.9 %copy-start.29 = (bf16[64]{0:T(256)(128)(2,1)S(1)}, bf16[64]{0:T(256)(128)(2,1)}, u32[]{:S(2)}) copy-start(bf16[64]{0:T(256)(128)(2,1)} %param.29) | copy-start | bytes 388
  8.9 20.9 %copy-start.30 = (bf16[64]{0:T(256)(128)(2,1)S(1)}, bf16[64]{0:T(256)(128)(2,1)}, u32[]{:S(2)}) copy-start(bf16[64]{0:T(256)(128)(2,1)} %param.33) | copy-start | bytes 388
  8.9 20.9 %copy-start.31 = (bf16[128]{0:T(256)(128)(2,1)S(1)}, bf16[128]{0:T(256)(128)(2,1)}, u32[]{:S(2)}) copy-start(bf16[128]{0:T(256)(128)(2,1)} %param.25) | copy-start | bytes 772
  8.9 20.9 %copy-start.32 = (bf16[256]{0:T(256)(128)(2,1)S(1)}, bf16[256]{0:T(256)(128)(2,1)}, u32[]{:S(2)}) copy-start(bf16[256]{0:T(256)(128)(2,1)} %param.31) | copy-start | bytes 1540
  24.5 109.8 %all-to-all-start = ((bf16[4,64,2048]{2,1,0:T(8,128)(2,1)}), bf16[4,64,2048]{2,1,0:T(8,128)(2,1)S(1)}, u32[]{:S(2)}, u32[]{:S(2)}) async-start(bf16[4,64,2048]{2,1,0:T(8,128)(2,1)} %bitcast), calls=%async_computation | async-start | bytes 2097152 | tf_op jit(solution)/shard_map/all_to_all | solution.py:382
  29.8 162.8 %all-gather.11.cloned.1.call-start = ((), (), s32[]{:S(2)}) async-start(), calls=%async_computation.16 | async-start | bytes 9437184 | tf_op jit(solution)/shard_map/all_gather | solution.py:571
  134.2 69.6 %copy-start.12 = (f32[2048]{0:T(1024)}, f32[2048]{0:T(1024)S(1)}, u32[]{:S(2)}) copy-start(f32[2048]{0:T(1024)S(1)} %reshape.398) | copy-start | bytes 24580
  134.6 69.2 %copy-start.18 = (f32[256]{0:T(256)}, f32[256]{0:T(256)S(1)}, u32[]{:S(2)}) copy-start(f32[256]{0:T(256)S(1)} %div.143) | copy-start | bytes 3076
  135.1 2.5 copy-start.22
  135.2 68.7 %copy-start.20 = (f32[256]{0:T(256)}, f32[256]{0:T(256)S(1)}, u32[]{:S(2)}) copy-start(f32[256]{0:T(256)S(1)} %rsqrt.21) | copy-start | bytes 3076
  136.6 124.9 %all-gather.15.cloned.1.call-start = ((), (), s32[]{:S(2)}) async-start(), calls=%async_computation.18 | async-start | bytes 2359296 | tf_op jit(solution)/shard_map/all_gather | solution.py:562
  137.4 203.1 %reduce-scatter.9.cloned.1.call-start = ((), (), s32[]{:S(2)}) async-start(), calls=%async_computation.19 | async-start | bytes 9437184 | tf_op jit(solution)/shard_map/reduce_scatter | solution.py:574
  261.5 7.2 copy-start.5
  268.7 1.2 copy-start.10
  268.7 172.7 %all-gather.19.cloned.1.call-start = ((), (), s32[]{:S(2)}) async-start(), calls=%async_computation.21 | async-start | bytes 5242880 | tf_op jit(solution)/shard_map/all_gather | solution.py:387
  289.0 210.2 %all-gather.17.cloned.1.call-start = ((), (), s32[]{:S(2)}) async-start(), calls=%async_computation.20 | async-start | bytes 9437184 | tf_op jit(solution)/shard_map/all_gather | solution.py:571
  340.4 3.7 copy-start.3
  342.2 4.4 copy-start.11
  345.8 233.3 %all-gather.21.cloned.1.call-start = ((), (), s32[]{:S(2)}) async-start(), calls=%async_computation.22 | async-start | bytes 5242880 | tf_op jit(solution)/shard_map/all_gather | solution.py:561
  346.5 289.7 %all-gather.23.cloned.1.call-start = ((), (), s32[]{:S(2)}) async-start(), calls=%async_computation.24 | async-start | bytes 9437184 | tf_op jit(solution)/shard_map/all_gather | solution.py:571
  402.8 339.0 %reduce-scatter.13.cloned.1.call-start = ((), (), s32[]{:S(2)}) async-start(), calls=%async_computation.25 | async-start | bytes 9437184 | tf_op jit(solution)/shard_map/reduce_scatter | solution.py:574
  636.2 22.6 %copy-start.33 = (bf16[2048,1024]{1,0:T(8,128)(2,1)S(1)}, bf16[2048,1024]{1,0:T(8,128)(2,1)}, u32[]{:S(2)}) copy-start(bf16[2048,1024]{1,0:T(8,128)(2,1)} %all-gather.19.cloned.1.call-done) | copy-start | bytes 12582916
  656.7 2.1 copy-start.34
  670.2 146.5 %reduce-scatter.11.cloned.1.call-start = ((), (), s32[]{:S(2)}) async-start(), calls=%async_computation.23 | async-start | bytes 9437184 | tf_op jit(solution)/shard_map/reduce_scatter | solution.py:574
  685.9 0.7 copy-start.14
  685.9 192.2 %all-gather.25.cloned.1.call-start = ((), (), s32[]{:S(2)}) async-start(), calls=%async_computation.26 | async-start | bytes 9437184 | tf_op jit(solution)/shard_map/all_gather | solution.py:571
  744.8 76.8 %copy-start.2 = (bf16[4,64,2048]{2,1,0:T(8,128)(2,1)S(1)}, bf16[4,64,2048]{2,1,0:T(8,128)(2,1)}, u32[]{:S(2)}) copy-start(bf16[4,64,2048]{2,1,0:T(8,128)(2,1)} %all_to_all.42) | copy-start | bytes 3145732
  820.3 1.3 copy-start.4
  823.7 186.5 %reduce-scatter.21.cloned.1.call-start = ((), (), s32[]{:S(2)}) async-start(), calls=%async_computation.30 | async-start | bytes 5242880 | tf_op jit(solution)/shard_map/reduce_scatter | solution.py:393
  837.9 196.3 %reduce-scatter.17.cloned.1.call-start = ((), (), s32[]{:S(2)}) async-start(), calls=%async_computation.28 | async-start | bytes 3932160 | tf_op jit(solution)/shard_map/reduce_scatter | solution.py:393
  960.9 1.6 copy-start.9
  972.9 135.3 %reduce-scatter.15.cloned.1.call-start = ((), (), s32[]{:S(2)}) async-start(), calls=%async_computation.27 | async-start | bytes 9437184 | tf_op jit(solution)/shard_map/reduce_scatter | solution.py:574
  984.9 224.8 %reduce-scatter.23.cloned.1.call-start = ((), (), s32[]{:S(2)}) async-start(), calls=%async_computation.31 | async-start | bytes 5242880 | tf_op jit(solution)/shard_map/reduce_scatter | solution.py:615
  1001.6 1.7 copy-start.6
  1001.6 278.4 %reduce-scatter.19.cloned.1.call-start = ((), (), s32[]{:S(2)}) async-start(), calls=%async_computation.29 | async-start | bytes 2359296 | tf_op jit(solution)/shard_map/reduce_scatter | solution.py:634
  1010.1 98.2 %copy-start.13 = (f32[2048]{0:T(1024)S(1)}, f32[2048]{0:T(1024)}, u32[]{:S(2)}) copy-start(f32[2048]{0:T(1024)} %copy-done.12) | copy-start | bytes 24580
  1010.1 98.2 %copy-start.19 = (f32[256]{0:T(256)S(1)}, f32[256]{0:T(256)}, u32[]{:S(2)}) copy-start(f32[256]{0:T(256)} %copy-done.18) | copy-start | bytes 3076
  1010.1 100.2 %copy-start.23 = (f32[256]{0:T(256)S(1)}, f32[256]{0:T(256)}, u32[]{:S(2)}) copy-start(f32[256]{0:T(256)} %copy-done.22) | copy-start | bytes 3076
  1010.1 100.2 %copy-start.21 = (f32[256]{0:T(256)S(1)}, f32[256]{0:T(256)}, u32[]{:S(2)}) copy-start(f32[256]{0:T(256)} %copy-done.20) | copy-start | bytes 3076
  1028.9 83.7 %all-to-all-start.3 = ((bf16[4,64,2048]{2,1,0:T(8,128)(2,1)}), bf16[4,64,2048]{2,1,0:T(8,128)(2,1)}, u32[]{:S(2)}, u32[]{:S(2)}) async-start(bf16[4,64,2048]{2,1,0:T(8,128)(2,1)} %bitcast.15), calls=%async_computation.5 | async-start | bytes 2097152 | tf_op jit(solution)/shard_map/all_to_all | solution.py:382
  1108.2 9.1 copy-start.7
  1112.6 15.2 %all-to-all-start.6 = ((bf16[4,128,768]{1,2,0:T(8,128)(2,1)}), bf16[4,128,768]{1,2,0:T(8,128)(2,1)}, u32[]{:S(2)}, u32[]{:S(2)}) async-start(bf16[4,128,768]{1,2,0:T(8,128)(2,1)} %copy.68), calls=%async_computation.11 | async-start | bytes 1572864 | tf_op jit(solution)/shard_map/all_to_all | solution.py:395
  1117.3 15.8 %copy-start.24 = (f32[1024]{0:T(1024)S(1)}, f32[1024]{0:T(1024)}, u32[]{:S(2)}) copy-start(f32[1024]{0:T(1024)} %get-tuple-element.452) | copy-start | bytes 12292
  1120.9 91.5 %copy-start.8 = (bf16[4,128,1024]{2,1,0:T(8,128)(2,1)S(1)}, bf16[4,128,1024]{2,1,0:T(8,128)(2,1)}, u32[]{:S(2)}) copy-start(bf16[4,128,1024]{2,1,0:T(8,128)(2,1)} %all_to_all.43) | copy-start | bytes 3145732
  1127.7 286.4 %all-to-all-start.5 = ((bf16[4,64,2048]{2,1,0:T(8,128)(2,1)}), bf16[4,64,2048]{2,1,0:T(8,128)(2,1)}, u32[]{:S(2)}, u32[]{:S(2)}) async-start(bf16[4,64,2048]{2,1,0:T(8,128)(2,1)} %bitcast.255), calls=%async_computation.9 | async-start | bytes 2097152 | tf_op jit(solution)/shard_map/all_to_all | solution.py:382
  1132.9 277.2 %all-reduce.3.cloned.1.call-start = ((), (), s32[]{:S(2)}) async-start(), calls=%async_computation.32 | async-start | bytes 196608
  1213.4 6.0 copy-start.16
  1213.4 6.1 copy-start.15
  1213.4 6.1 copy-start.17
  1283.9 134.8 %copy-start.1 = (s32[4,2]{0,1:T(2,128)S(1)}, s32[4,2]{0,1:T(2,128)}, u32[]{:S(2)}) copy-start(s32[4,2]{0,1:T(2,128)} %param.20) | copy-start | bytes 100
Sparse Core Ops, SparseCore 0:
  24.6 77.2 all-gather.12
  136.7 55.8 all-gather.10
  194.8 48.2 all-gather.14
  268.9 71.5 reduce-scatter.8
  342.4 98.9 all-gather.18
  443.7 55.4 all-gather.16
  500.7 78.2 all-gather.20
  580.9 55.1 all-gather.22
  670.3 71.4 reduce-scatter.12
  745.1 71.4 reduce-scatter.10
  823.8 54.2 all-gather.24
  880.2 76.7 reduce-scatter.20
  973.0 59.7 reduce-scatter.16
  1036.2 72.0 reduce-scatter.14
  1110.4 99.2 reduce-scatter.22
  1213.0 66.8 reduce-scatter.18
  1286.0 123.9 all-reduce.2

commit v2 on v1

--- a/solution.py
+++ b/solution.py
@@ -1,8 +1,11 @@
+import functools
 import math
 
 import jax
 import jax.numpy as jnp
 from jax import lax
+from jax.experimental import pallas as pl
+from jax.experimental.pallas import tpu as pltpu
 from jax.sharding import Mesh
 from jax.sharding import PartitionSpec as P
 
@@ -378,106 +381,493 @@
     )
 
 
-def spread_rows(rows):
-    return lax.all_to_all(rows, "z", split_axis=0, concat_axis=0, tiled=True)
-
-
-def gather_columns(blocks):
-    turned = lax.all_to_all(blocks, ("y", "x"), split_axis=0, concat_axis=0, tiled=True)
-    return lax.all_gather(
-        turned.reshape(-1, turned.shape[2]), "z", axis=0, tiled=True
-    )
-
-
-def scatter_columns(term, plane):
-    own = lax.psum_scatter(term, "z", scatter_dimension=0, tiled=True)
-    blocks = own.reshape(plane, own.shape[0] // plane, own.shape[1])
-    return lax.all_to_all(blocks, ("y", "x"), split_axis=0, concat_axis=0, tiled=True)
-
-
-def token_positions(index, rows_y, rows_x, depth, seq_rows):
+CHUNKS = 4
+LOG2E = 1.4426950408889634
+MESH = pl.DeviceIdType.MESH
+
+
+def remote(src, dst, send, recv, peer):
+    return pltpu.make_async_remote_copy(
+        src_ref=src,
+        dst_ref=dst,
+        send_sem=send,
+        recv_sem=recv,
+        device_id=peer,
+        device_id_type=MESH,
+    )
+
+
+def greet(peers):
+    barrier = pltpu.get_barrier_semaphore()
+    for peer in peers:
+        pl.semaphore_signal(barrier, inc=1, device_id=peer, device_id_type=MESH)
+    pl.semaphore_wait(barrier, len(peers))
+
+
+class Corner:
+    def __init__(self):
+        self.c = lax.axis_index("dp")
+        self.y = lax.axis_index("y")
+        self.x = lax.axis_index("x")
+        self.ax = self.x + (1 - self.c) * (1 - 2 * self.x)
+        self.ay = self.y + self.c * (1 - 2 * self.y)
+        self.bx = self.x + self.c * (1 - 2 * self.x)
+        self.by = self.y + (1 - self.c) * (1 - 2 * self.y)
+        self.dx = 1 - self.x
+        self.dy = 1 - self.y
+        self.peer_a = {"y": self.ay, "x": self.ax}
+        self.peer_b = {"y": self.by, "x": self.bx}
+        self.sibling = {"dp": 1 - self.c}
+
+    def slots(self, core):
+        return [
+            (core * 2 + y) * 2 + x
+            for y, x in (
+                (self.dy, self.dx),
+                (self.by, self.bx),
+                (self.ay, self.ax),
+                (self.y, self.x),
+            )
+        ]
+
+
+def gather_kernel(rows_ref, all_ref, local_sem, send, recv):
+    at = Corner()
+    slot_d, slot_b, slot_a, me = at.slots(at.c)
+    step = rows_ref.shape[0] // CHUNKS
+    greet([at.peer_a, at.peer_b, at.sibling])
+    local = pltpu.make_async_copy(rows_ref, all_ref.at[me], local_sem)
+    local.start()
+
+    def copy(kind, k, slot, peer):
+        part = pl.ds(k * step, step)
+        src = rows_ref.at[part] if kind < 3 else all_ref.at[slot, part]
+        return remote(src, all_ref.at[slot, part], send.at[kind, k], recv.at[kind, k], peer)
+
+    def arrived(kind, k, slot, peer):
+        part = pl.ds(k * step, step)
+        block = all_ref.at[slot, part]
+        remote(block, block, send.at[kind, k], recv.at[kind, k], peer).wait_recv()
+
+    sent = []
+
+    def start(kind, k, slot, peer):
+        one = copy(kind, k, slot, peer)
+        one.start()
+        sent.append(one)
+
+    for k in range(CHUNKS):
+        start(0, k, me, at.peer_a)
+        start(1, k, me, at.peer_b)
+    for k in range(CHUNKS):
+        start(2, k, me, at.sibling)
+    for k in range(CHUNKS):
+        arrived(0, k, slot_a, at.peer_a)
+        start(3, k, slot_a, at.peer_b)
+        start(4, k, slot_a, at.sibling)
+    for k in range(CHUNKS):
+        arrived(1, k, slot_b, at.peer_b)
+        start(5, k, slot_b, at.sibling)
+    for k in range(CHUNKS):
+        arrived(3, k, slot_d, at.peer_b)
+        start(6, k, slot_d, at.sibling)
+    other_d, other_b, other_a, other_me = at.slots(1 - at.c)
+    for k in range(CHUNKS):
+        arrived(2, k, other_me, at.sibling)
+        arrived(4, k, other_b, at.sibling)
+        arrived(5, k, other_a, at.sibling)
+        arrived(6, k, other_d, at.sibling)
+    for one in sent:
+        one.wait_send()
+    local.wait()
+
+
+def gather_tokens(rows):
+    count, width = rows.shape
+    return pl.pallas_call(
+        gather_kernel,
+        out_shape=jax.ShapeDtypeStruct((8, count, width), rows.dtype),
+        in_specs=[pl.BlockSpec(memory_space=pl.ANY)],
+        out_specs=pl.BlockSpec(memory_space=pl.ANY),
+        scratch_shapes=[
+            pltpu.SemaphoreType.DMA,
+            pltpu.SemaphoreType.DMA((7, CHUNKS)),
+            pltpu.SemaphoreType.DMA((7, CHUNKS)),
+        ],
+        compiler_params=pltpu.CompilerParams(collective_id=1, has_side_effects=True),
+        cost_estimate=pl.CostEstimate(
+            flops=0, bytes_accessed=16 * count * width * 4, transcendentals=0
+        ),
+        name="gather_tokens",
+    )(rows).reshape(8 * count, width)
+
+
+def scatter_kernel(part_ref, own_ref, from_core, from_b, from_a, send, recv):
+    at = Corner()
+    slot_d, slot_b, slot_a, me = at.slots(at.c)
+    other_d, other_b, other_a, other_me = at.slots(1 - at.c)
+    step = own_ref.shape[0] // CHUNKS
+    wide = jnp.float32
+    greet([at.peer_a, at.peer_b, at.sibling])
+    sent = []
+
+    def start(kind, k, src, dst, peer):
+        one = remote(src, dst, send.at[kind, k], recv.at[kind, k], peer)
+        one.start()
+        sent.append(one)
+
+    def arrived(kind, k, dst, peer):
+        remote(dst, dst, send.at[kind, k], recv.at[kind, k], peer).wait_recv()
+
+    for q, slot in enumerate((other_d, other_a, other_b, other_me)):
+        for k in range(CHUNKS):
+            part = pl.ds(k * step, step)
+            start(q, k, part_ref.at[slot, part], from_core.at[q, part], at.sibling)
+    for q, slot in enumerate((slot_d, slot_b)):
+        for k in range(CHUNKS):
+            part = pl.ds(k * step, step)
+            arrived(q, k, from_core.at[q, part], at.sibling)
+            total = part_ref[slot, part].astype(wide) + from_core[q, part].astype(wide)
+            from_core[q, part] = total.astype(from_core.dtype)
+            start(4 + q, k, from_core.at[q, part], from_b.at[q, part], at.peer_b)
+    for k in range(CHUNKS):
+        part = pl.ds(k * step, step)
+        arrived(2, k, from_core.at[2, part], at.sibling)
+        arrived(4, k, from_b.at[0, part], at.peer_b)
+        total = part_ref[slot_a, part].astype(wide) + from_core[2, part].astype(wide)
+        total = total + from_b[0, part].astype(wide)
+        from_core[2, part] = total.astype(from_core.dtype)
+        start(6, k, from_core.at[2, part], from_a.at[part], at.peer_a)
+    for k in range(CHUNKS):
+        part = pl.ds(k * step, step)
+        arrived(3, k, from_core.at[3, part], at.sibling)
+        arrived(5, k, from_b.at[1, part], at.peer_b)
+        arrived(6, k, from_a.at[part], at.peer_a)
+        total = part_ref[me, part].astype(wide) + from_core[3, part].astype(wide)
+        total = total + from_b[1, part].astype(wide)
+        own_ref[part] = total + from_a[part].astype(wide)
+    for one in sent:
+        one.wait_send()
+
+
+def scatter_tokens(partial):
+    count, width = partial.shape[0] // 8, partial.shape[1]
+    return pl.pallas_call(
+        scatter_kernel,
+        out_shape=jax.ShapeDtypeStruct((count, width), jnp.float32),
+        in_specs=[pl.BlockSpec(memory_space=pltpu.VMEM)],
+        out_specs=pl.BlockSpec(memory_space=pltpu.VMEM),
+        scratch_shapes=[
+            pltpu.VMEM((4, count, width), partial.dtype),
+            pltpu.VMEM((2, count, width), partial.dtype),
+            pltpu.VMEM((count, width), partial.dtype),
+            pltpu.SemaphoreType.DMA((7, CHUNKS)),
+            pltpu.SemaphoreType.DMA((7, CHUNKS)),
+        ],
+        compiler_params=pltpu.CompilerParams(
+            collective_id=2, has_side_effects=True, vmem_limit_bytes=40 * 2**20
+        ),
+        cost_estimate=pl.CostEstimate(
+            flops=0, bytes_accessed=16 * count * width * 4, transcendentals=0
+        ),
+        name="scatter_tokens",
+    )(partial.reshape(8, count, width))
+
+
+def exchange_kernel(n_deep, n_flat, gathers, reduces, *refs):
+    refs = list(refs)
+    take = lambda n: [refs.pop(0) for _ in range(n)]
+    deep_in, flat_in = take(n_deep), take(n_flat)
+    vec_in = take(gathers + reduces)
+    deep_out, flat_out = take(n_deep), take(n_flat)
+    vec_out = take(gathers + reduces)
+    near = take(reduces)
+    far = take(reduces)
+    here = take(reduces)
+    send, recv = take(2)
+    c, z = lax.axis_index("dp"), lax.axis_index("z")
+    place = lax.axis_index("y") * 2 + lax.axis_index("x")
+    rank = c * 4 + place
+
+    def deep(i):
+        return lax.rem(z + i, 4)
+
+    def flat(i):
+        return lax.rem(place + i, 4)
+
+    def wide(i):
+        return lax.rem(rank + i, 8)
+
+    def deep_peer(i):
+        return {"z": deep(i)}
+
+    def flat_peer(i):
+        return {"y": flat(i) // 2, "x": lax.rem(flat(i), 2)}
+
+    def wide_peer(i):
+        return {
+            "dp": wide(i) // 4,
+            "y": lax.rem(wide(i), 4) // 2,
+            "x": lax.rem(wide(i), 2),
+        }
+
+    others = range(1, 4)
+    peers = []
+    if n_deep or gathers or reduces:
+        peers += [deep_peer(i) for i in others]
+    if gathers or reduces:
+        peers += [wide_peer(i) for i in range(1, 8)]
+    elif n_flat:
+        peers += [flat_peer(i) for i in others]
+    greet(peers)
+    sent, waits = [], []
+    count = [0]
+
+    def post(src, dst, peer, landing):
+        k = count[0]
+        count[0] += 1
+        one = remote(src, dst, send.at[k], recv.at[k], peer)
+        one.start()
+        sent.append(one)
+        return remote(landing, landing, send.at[k], recv.at[k], peer)
+
+    stage = []
+    for i in range(1, 8) if gathers or reduces else ():
+        if gathers:
+            stage.append(
+                post(
+                    vec_in[0], vec_out[0].at[z, rank], wide_peer(i), vec_out[0].at[z, wide(8 - i)]
+                )
+            )
+        else:
+            stage.append(
+                post(vec_in[0].at[wide(i)], near[0].at[rank], wide_peer(i), near[0].at[wide(8 - i)])
+            )
+    for index, me, peer, ins, outs in (
+        (deep, z, deep_peer, deep_in, deep_out),
+        (flat, place, flat_peer, flat_in, flat_out),
+    ):
+        for src, dst in zip(ins, outs):
+            for i in others:
+                waits.append(post(src.at[index(i)], dst.at[me], peer(i), dst.at[index(4 - i)]))
+    for me, ins, outs in ((z, deep_in, deep_out), (place, flat_in, flat_out)):
+        for src, dst in zip(ins, outs):
+            dst[me] = src[me]
+    if gathers:
+        vec_out[0][z, rank] = vec_in[0][...]
+        for one in stage:
+            one.wait_recv()
+        for i in others:
+            waits.append(
+                post(vec_out[0].at[z], vec_out[0].at[z], deep_peer(i), vec_out[0].at[deep(4 - i)])
+            )
+    if reduces:
+        near[0][rank] = vec_in[0][rank]
+        for one in stage:
+            one.wait_recv()
+        here[0][...] = jnp.sum(near[0][...], 0)
+        last = []
+        for i in others:
+            last.append(
+                post(here[0].at[deep(i)], far[0].at[z], deep_peer(i), far[0].at[deep(4 - i)])
+            )
+        far[0][z] = here[0][z]
+        for one in last:
+            one.wait_recv()
+        vec_out[0][...] = jnp.sum(far[0][...], 0)
+    for one in waits:
+        one.wait_recv()
+    for one in sent:
+        one.wait_send()
+
+
+def exchange(identity, deep, flat, gathered=None, reduced=None):
+    vectors = [v for v in (gathered, reduced) if v is not None]
+    shapes = [jax.ShapeDtypeStruct(a.shape, a.dtype) for a in (*deep, *flat)]
+    scratch = []
+    copies = 3 * (len(deep) + len(flat))
+    if gathered is not None:
+        shapes.append(jax.ShapeDtypeStruct((4, 8) + gathered.shape, gathered.dtype))
+    if reduced is not None:
+        tile = reduced.shape[2:]
+        shapes.append(jax.ShapeDtypeStruct(tile, reduced.dtype))
+        scratch = [
+            pltpu.VMEM((8, 4) + tile, reduced.dtype),
+            pltpu.VMEM((4,) + tile, reduced.dtype),
+            pltpu.VMEM((4,) + tile, reduced.dtype),
+        ]
+    copies += 10 * len(vectors)
+    operands = [*deep, *flat, *vectors]
+    moved = sum(a.size * a.dtype.itemsize for a in operands)
+    return pl.pallas_call(
+        functools.partial(
+            exchange_kernel, len(deep), len(flat), int(gathered is not None), int(reduced is not None)
+        ),
+        out_shape=shapes,
+        in_specs=[pl.BlockSpec(memory_space=pltpu.VMEM)] * len(operands),
+        out_specs=[pl.BlockSpec(memory_space=pltpu.VMEM)] * len(shapes),
+        scratch_shapes=scratch
+        + [pltpu.SemaphoreType.DMA((copies,)), pltpu.SemaphoreType.DMA((copies,))],
+        compiler_params=pltpu.CompilerParams(
+            collective_id=identity, has_side_effects=True, vmem_limit_bytes=40 * 2**20
+        ),
+        cost_estimate=pl.CostEstimate(flops=0, bytes_accessed=16 * moved, transcendentals=0),
+        name=f"exchange_{identity}",
+    )(*operands)
+
+
+def scores_of(item_ref, first, block, slope, prefix, depth, seq_rows):
+    length = item_ref.shape[0]
+    head_dim = item_ref.shape[1] // 3
     own_rows = depth * seq_rows
-    chip = index // own_rows
-    block = index % own_rows // seq_rows
-    return (block * (rows_y * rows_x) + chip) * seq_rows + index % seq_rows
-
-
-def attend_forward(
-    projected, slopes, prefixes, cores, own_heads, head_dim, rows_y, rows_x, depth, seq_rows
+    chips = length // own_rows
+
+    def position(index):
+        chip = index // own_rows
+        rest = index % own_rows
+        return ((rest // seq_rows) * chips + chip) * seq_rows + rest % seq_rows
+
+    queries = item_ref[first : first + block, :head_dim]
+    keys = item_ref[:, head_dim : 2 * head_dim]
+    raw = lax.dot_general(
+        keys, queries, (((1,), (1,)), ((), ())), preferred_element_type=jnp.float32
+    )
+    key_pos = position(lax.broadcasted_iota(jnp.int32, (length, 1), 0))
+    query_pos = position(first + lax.broadcasted_iota(jnp.int32, (1, block), 1))
+    bound = jnp.where(key_pos < prefix, -1, key_pos)
+    distance = jnp.abs(
+        query_pos.astype(jnp.float32) - key_pos.astype(jnp.float32)
+    )
+    scores = raw * (LOG2E / math.sqrt(head_dim)) - (slope * LOG2E) * distance
+    return jnp.where(bound <= query_pos, scores, jnp.float32(-1e30))
+
+
+def forward_kernel(depth, seq_rows, block, prefix_ref, slope_ref, item_ref, mixed_ref, total_ref):
+    prefix = prefix_ref[pl.program_id(0)]
+    slope = slope_ref[pl.program_id(1)]
+    length = item_ref.shape[0]
+    head_dim = item_ref.shape[1] // 3
+    for first in range(0, length, block):
+        scores = scores_of(item_ref, first, block, slope, prefix, depth, seq_rows)
+        top = jnp.max(scores, 0, keepdims=True)
+        powers = jnp.exp2(scores - top)
+        total = jnp.sum(powers, 0, keepdims=True)
+        probs = (powers * (1.0 / total)).astype(jnp.bfloat16)
+        mixed = lax.dot_general(
+            probs,
+            item_ref[:, 2 * head_dim :],
+            (((0,), (0,)), ((), ())),
+            preferred_element_type=jnp.float32,
+        )
+        mixed_ref[first : first + block, :] = mixed.astype(mixed_ref.dtype)
+        total_ref[0, :, first : first + block] = top + jnp.log2(total)
+
+
+def attend_forward(projected, slopes, prefixes, own_heads, head_dim, depth, seq_rows):
+    cores = prefixes.shape[0]
+    length = projected.shape[0] // cores
+    block = min(256, length)
+    scores = cores * own_heads * length * length
+    return pl.pallas_call(
+        functools.partial(forward_kernel, depth, seq_rows, block),
+        grid=(cores, own_heads),
+        out_shape=[
+            jax.ShapeDtypeStruct((cores * length, own_heads * head_dim), projected.dtype),
+            jax.ShapeDtypeStruct((cores * own_heads, 1, length), jnp.float32),
+        ],
+        in_specs=[
+            pl.BlockSpec(memory_space=pltpu.SMEM),
+            pl.BlockSpec(memory_space=pltpu.SMEM),
+            pl.BlockSpec((length, 3 * head_dim), lambda s, h: (s, h)),
+        ],
+        out_specs=[
+            pl.BlockSpec((length, head_dim), lambda s, h: (s, h)),
+            pl.BlockSpec((1, 1, length), lambda s, h: (s * own_heads + h, 0, 0)),
+        ],
+        compiler_params=pltpu.CompilerParams(vmem_limit_bytes=48 * 2**20),
+        cost_estimate=pl.CostEstimate(
+            flops=4 * scores * head_dim,
+            bytes_accessed=2 * projected.size * 2,
+            transcendentals=scores,
+        ),
+        name="attend_forward",
+    )(prefixes, slopes, projected)
+
+
+def backward_kernel(
+    depth, seq_rows, block, prefix_ref, slope_ref, item_ref, grad_ref, total_ref, out_ref, key_sum, value_sum
 ):
+    prefix = prefix_ref[pl.program_id(0)]
+    slope = slope_ref[pl.program_id(1)]
+    length = item_ref.shape[0]
+    head_dim = item_ref.shape[1] // 3
+    scale = 1.0 / math.sqrt(head_dim)
+    half = jnp.bfloat16
     wide = jnp.float32
+    for first in range(0, length, block):
+        scores = scores_of(item_ref, first, block, slope, prefix, depth, seq_rows)
+        probs = jnp.exp2(scores - total_ref[0, :, first : first + block])
+        grad = grad_ref[first : first + block, :]
+        grad_probs = lax.dot_general(
+            item_ref[:, 2 * head_dim :],
+            grad,
+            (((1,), (1,)), ((), ())),
+            preferred_element_type=wide,
+        )
+        inner = jnp.sum(grad_probs * probs, 0, keepdims=True)
+        grad_scores = (probs * (grad_probs - inner)).astype(half)
+        key_term = jnp.dot(
+            grad_scores, item_ref[first : first + block, :head_dim], preferred_element_type=wide
+        )
+        value_term = jnp.dot(probs.astype(half), grad, preferred_element_type=wide)
+        query_grad = lax.dot_general(
+            grad_scores,
+            item_ref[:, head_dim : 2 * head_dim],
+            (((0,), (0,)), ((), ())),
+            preferred_element_type=wide,
+        )
+        out_ref[first : first + block, :head_dim] = (query_grad * scale).astype(half)
+        if first == 0:
+            key_sum[...] = key_term
+            value_sum[...] = value_term
+        else:
+            key_sum[...] += key_term
+            value_sum[...] += value_term
+    out_ref[:, head_dim : 2 * head_dim] = (key_sum[...] * scale).astype(half)
+    out_ref[:, 2 * head_dim :] = value_sum[...].astype(half)
+
+
+def attend_backward(
+    projected, grad_mixed, totals, slopes, prefixes, own_heads, head_dim, depth, seq_rows
+):
+    cores = prefixes.shape[0]
     length = projected.shape[0] // cores
-    scale = 1.0 / math.sqrt(head_dim)
-    grouped = projected.reshape(cores, length, own_heads, 3, head_dim)
-    pos = token_positions(
-        jnp.arange(length, dtype=jnp.int32), rows_y, rows_x, depth, seq_rows
-    )
-
-    def one(pair):
-        seq, head = pair // own_heads, pair % own_heads
-        item = grouped[seq, :, head]
-        scores = jnp.einsum("qe,ke->qk", item[:, 0], item[:, 1], preferred_element_type=wide)
-        distance = jnp.abs(pos[:, None] - pos[None, :]).astype(wide)
-        scores = scores * scale - slopes[head] * distance
-        allowed = (pos[None, :] <= pos[:, None]) | (pos[None, :] < prefixes[seq])
-        scores = jnp.where(allowed, scores, jnp.float32(-1e30))
-        row_max = jnp.max(scores, -1, keepdims=True)
-        powers = jnp.exp(scores - row_max)
-        total = jnp.sum(powers, -1, keepdims=True)
-        probs = (powers / total).astype(jnp.bfloat16)
-        mixed = jnp.dot(probs, item[:, 2], preferred_element_type=wide).astype(jnp.bfloat16)
-        return mixed, (row_max + jnp.log(total))[:, 0]
-
-    mixed, totals = lax.map(one, jnp.arange(cores * own_heads, dtype=jnp.int32))
-    mixed = mixed.reshape(cores, own_heads, length, head_dim).transpose(0, 2, 1, 3)
-    return mixed.reshape(cores * length, own_heads * head_dim), totals
-
-
-def attend_backward(
-    projected,
-    grad_mixed,
-    totals,
-    slopes,
-    prefixes,
-    cores,
-    own_heads,
-    head_dim,
-    rows_y,
-    rows_x,
-    depth,
-    seq_rows,
-):
-    wide = jnp.float32
-    half = jnp.bfloat16
-    length = projected.shape[0] // cores
-    scale = 1.0 / math.sqrt(head_dim)
-    grouped = projected.reshape(cores, length, own_heads, 3, head_dim)
-    upstream = grad_mixed.reshape(cores, length, own_heads, head_dim)
-    pos = token_positions(
-        jnp.arange(length, dtype=jnp.int32), rows_y, rows_x, depth, seq_rows
-    )
-
-    def one(pair):
-        seq, head = pair // own_heads, pair % own_heads
-        item = grouped[seq, :, head]
-        grad = upstream[seq, :, head]
-        scores = jnp.einsum("qe,ke->qk", item[:, 0], item[:, 1], preferred_element_type=wide)
-        distance = jnp.abs(pos[:, None] - pos[None, :]).astype(wide)
-        scores = scores * scale - slopes[head] * distance
-        allowed = (pos[None, :] <= pos[:, None]) | (pos[None, :] < prefixes[seq])
-        scores = jnp.where(allowed, scores, jnp.float32(-1e30))
-        probs = jnp.exp(scores - totals[pair][:, None])
-        grad_probs = jnp.einsum("qe,ke->qk", grad, item[:, 2], preferred_element_type=wide)
-        inner = jnp.sum(grad_probs * probs, -1, keepdims=True)
-        grad_scores = (probs * (grad_probs - inner)).astype(half)
-        query = jnp.dot(grad_scores, item[:, 1], preferred_element_type=wide) * scale
-        key = jnp.einsum("qk,qe->ke", grad_scores, item[:, 0], preferred_element_type=wide) * scale
-        value = jnp.einsum("qk,qe->ke", probs.astype(half), grad, preferred_element_type=wide)
-        return jnp.stack([query, key, value], 1).astype(half)
-
-    grads = lax.map(one, jnp.arange(cores * own_heads, dtype=jnp.int32))
-    grads = grads.reshape(cores, own_heads, length, 3, head_dim).transpose(0, 2, 1, 3, 4)
-    return grads.reshape(cores * length, own_heads * 3 * head_dim)
+    block = min(256, length)
+    scores = cores * own_heads * length * length
+    return pl.pallas_call(
+        functools.partial(backward_kernel, depth, seq_rows, block),
+        grid=(cores, own_heads),
+        out_shape=jax.ShapeDtypeStruct(projected.shape, projected.dtype),
+        in_specs=[
+            pl.BlockSpec(memory_space=pltpu.SMEM),
+            pl.BlockSpec(memory_space=pltpu.SMEM),
+            pl.BlockSpec((length, 3 * head_dim), lambda s, h: (s, h)),
+            pl.BlockSpec((length, head_dim), lambda s, h: (s, h)),
+            pl.BlockSpec((1, 1, length), lambda s, h: (s * own_heads + h, 0, 0)),
+        ],
+        out_specs=pl.BlockSpec((length, 3 * head_dim), lambda s, h: (s, h)),
+        scratch_shapes=[
+            pltpu.VMEM((length, head_dim), jnp.float32),
+            pltpu.VMEM((length, head_dim), jnp.float32),
+        ],
+        compiler_params=pltpu.CompilerParams(vmem_limit_bytes=48 * 2**20),
+        cost_estimate=pl.CostEstimate(
+            flops=10 * scores * head_dim,
+            bytes_accessed=2 * projected.size * 2,
+            transcendentals=scores,
+        ),
+        name="attend_backward",
+    )(prefixes, slopes, projected, grad_mixed, totals)
 
 
 def planar(
@@ -513,13 +903,11 @@
     head_dim = triple_weight.shape[3]
     heads = triple_weight.shape[1]
     own_heads = heads // plane
-    length = seq_rows * depth * plane
     own_rows = seq_rows * depth
     units = expand_weight.shape[1]
     own_units = units // plane
     row_block = expand_weight.shape[0]
     shrink_rows = shrink_weight.shape[0]
-    group = ("dp", "y", "x")
 
     pieces = [
         first_gain,
@@ -531,9 +919,30 @@
         pair_bias,
         expand_shift,
     ]
-    packed = lax.all_gather(
-        jnp.concatenate(pieces), ("dp", "z", "y", "x"), axis=0, tiled=False
-    ).reshape(-1, sum(p.shape[0] for p in pieces))
+    piece_total = sum(p.shape[0] for p in pieces)
+    lanes = 128
+    vector_rows = -(-piece_total // (lanes * 16)) * 16
+    vector_tile = jnp.pad(
+        jnp.concatenate(pieces), (0, vector_rows * lanes - piece_total)
+    ).reshape(vector_rows, lanes)
+    triple_blocks = (
+        triple_weight.reshape(row_block, rows_x, own_heads, rows_y, 3 * head_dim)
+        .transpose(3, 1, 0, 2, 4)
+        .reshape(plane, row_block, own_heads * 3 * head_dim)
+    )
+    expand_blocks = (
+        expand_weight.reshape(row_block, depth, plane, shrink_rows)
+        .transpose(2, 0, 1, 3)
+        .reshape(plane, row_block, own_units)
+    )
+    inputs, upstream, triple_turned, expand_turned, packed = exchange(
+        3, (hidden[:, 0], cotangent[:, 0]), (triple_blocks, expand_blocks), gathered=vector_tile
+    )
+    packed = (
+        packed.reshape(depth, cores, plane, vector_rows * lanes)
+        .transpose(1, 0, 2, 3)
+        .reshape(-1, vector_rows * lanes)
+    )
     vectors = []
     offset = 0
     for piece in pieces:
@@ -548,15 +957,11 @@
     ).reshape(-1)
     unit_bias = unit_full.reshape(cores, depth, plane, shrink_rows)[core, :, place].reshape(-1)
 
-    triple_own = gather_columns(
-        triple_weight.reshape(row_block, rows_x, own_heads, rows_y, 3 * head_dim)
-        .transpose(3, 1, 0, 2, 4)
-        .reshape(plane, row_block, own_heads * 3 * head_dim)
-    )
-    expand_own = gather_columns(
-        expand_weight.reshape(row_block, depth, plane, shrink_rows)
-        .transpose(2, 0, 1, 3)
-        .reshape(plane, row_block, own_units)
+    triple_own = lax.all_gather(
+        triple_turned.reshape(-1, triple_turned.shape[2]), "z", axis=0, tiled=True
+    )
+    expand_own = lax.all_gather(
+        expand_turned.reshape(-1, expand_turned.shape[2]), "z", axis=0, tiled=True
     )
     shrink_own = lax.all_gather(shrink_weight, "z", axis=0, tiled=True)
     dense_rows = lax.all_gather(dense_weight, ("z", "x"), axis=0, tiled=True)
@@ -564,14 +969,8 @@
         dense_rows, at_x * own_heads * head_dim, own_heads * head_dim, 0
     )
 
-    inputs = spread_rows(hidden[:, 0]).reshape(own_rows, width).astype(wide)
-    upstream = spread_rows(cotangent[:, 0]).reshape(own_rows, width)
-
-    def gather_tokens(rows):
-        return lax.all_gather(rows, group, axis=0, tiled=True)
-
-    def scatter_tokens(partial):
-        return lax.psum_scatter(partial, group, scatter_dimension=0, tiled=True).astype(wide)
+    inputs = inputs.reshape(own_rows, width).astype(wide)
+    upstream = upstream.reshape(own_rows, width)
 
     normed_own = layer_norm(inputs, gain_one, shift_one).astype(half)
     normed = gather_tokens(normed_own)
@@ -587,7 +986,7 @@
     at_z = lax.axis_index("z")
     prefixes = lax.dynamic_index_in_dim(prefix_lengths, at_z, 0, False)
     mixed, log_totals = attend_forward(
-        projected, slopes, prefixes, cores, own_heads, head_dim, rows_y, rows_x, depth, seq_rows
+        projected, slopes, prefixes, own_heads, head_dim, depth, seq_rows
     )
     dense_part = jnp.dot(mixed, dense_own, preferred_element_type=wide).astype(half)
     middle = inputs + scatter_tokens(dense_part) + dense_bias
@@ -598,7 +997,6 @@
     activated = activated.astype(half)
     feed_part = jnp.dot(activated, shrink_own, preferred_element_type=wide).astype(half)
     layer_output = (middle + scatter_tokens(feed_part) + shrink_bias).astype(half)
-    layer_output = spread_rows(layer_output.reshape(depth, seq_rows, width))[:, None]
 
     grad_act = jnp.einsum("tf,uf->tu", upstream_all, shrink_own, preferred_element_type=wide)
     grad_pre = gelu_pull(grad_act)[0].astype(half)
@@ -616,14 +1014,7 @@
     expand_term = jnp.einsum(
         "td,tu->du", normed_two, grad_pre, preferred_element_type=wide
     ).astype(half)
-    expand_grad = (
-        scatter_columns(expand_term, plane)
-        .reshape(plane, row_block, depth, shrink_rows)
-        .transpose(1, 2, 0, 3)
-        .reshape(row_block, units)
-        .astype(wide)
-    )
-
+    expand_turned = lax.psum_scatter(expand_term, "z", scatter_dimension=0, tiled=True)
     grad_mixed = jnp.einsum("tf,ef->te", branch, dense_own, preferred_element_type=wide).astype(
         half
     )
@@ -640,11 +1031,8 @@
         log_totals,
         slopes,
         prefixes,
-        cores,
         own_heads,
         head_dim,
-        rows_y,
-        rows_x,
         depth,
         seq_rows,
     )
@@ -655,17 +1043,10 @@
         layer_norm, inputs, gain_one, shift_one
     )[1](scatter_tokens(norm_one_part))
     hidden_grad = (grad_middle + grad_norm_one).astype(half)
-    hidden_grad = spread_rows(hidden_grad.reshape(depth, seq_rows, width))[:, None]
     triple_term = jnp.einsum(
         "td,tc->dc", normed, grad_project, preferred_element_type=wide
     ).astype(half)
-    triple_grad = (
-        scatter_columns(triple_term, plane)
-        .reshape(rows_y, rows_x, row_block, own_heads, 3 * head_dim)
-        .transpose(2, 1, 3, 0, 4)
-        .reshape(row_block, heads, 3, head_dim)
-        .astype(wide)
-    )
+    triple_turned = lax.psum_scatter(triple_term, "z", scatter_dimension=0, tiled=True)
 
     head_sums = jnp.sum(grad_project, 0, dtype=wide).reshape(own_heads, 3, head_dim)
     pair_term = jnp.stack([head_sums[:, 0], head_sums[:, 2]], 1)
@@ -688,12 +1069,38 @@
         unit_wide,
     ]
     devices = cores * depth * plane
-    summed = lax.psum_scatter(
+    term_rows = -(-piece_total // (lanes * 8)) * 8
+    term_tiles = jnp.pad(
         jnp.concatenate([t.reshape(devices, -1) for t in terms], 1),
-        ("dp", "z", "y", "x"),
-        scatter_dimension=0,
-        tiled=True,
-    ).reshape(-1)
+        ((0, 0), (0, term_rows * lanes - piece_total)),
+    )
+    term_tiles = (
+        term_tiles.reshape(cores, depth, plane, term_rows, lanes)
+        .transpose(0, 2, 1, 3, 4)
+        .reshape(cores * plane, depth, term_rows, lanes)
+    )
+    layer_output, hidden_grad, expand_grad, summed = exchange(
+        4,
+        (layer_output.reshape(depth, seq_rows, width), hidden_grad.reshape(depth, seq_rows, width)),
+        (expand_turned.reshape(plane, row_block, own_units),),
+        reduced=term_tiles,
+    )
+    layer_output = layer_output[:, None]
+    hidden_grad = hidden_grad[:, None]
+    expand_grad = (
+        expand_grad.reshape(plane, row_block, depth, shrink_rows)
+        .transpose(1, 2, 0, 3)
+        .reshape(row_block, units)
+        .astype(wide)
+    )
+    (triple_grad,) = exchange(5, (), (triple_turned.reshape(plane, row_block, -1),))
+    triple_grad = (
+        triple_grad.reshape(rows_y, rows_x, row_block, own_heads, 3 * head_dim)
+        .transpose(2, 1, 3, 0, 4)
+        .reshape(row_block, heads, 3, head_dim)
+        .astype(wide)
+    )
+    summed = summed.reshape(-1)
     vector_grads = []
     offset = 0
     for piece in pieces:

time: 1430 us -> 872 us (0.61)
  waiting for transfers between devices: 828 us -> 130 us
  Pallas kernels: 0 us -> 519 us
  blocking collectives: 210 us -> 0 us
  matrix products: 184 us -> 133 us
  local copies, waits for them, and re-layouts: 88.7 us -> 47.8 us
  other arithmetic: 52.1 us -> 19.7 us
  loops' own time: 26.6 us -> 0 us
  starting transfers between devices: 21.3 us -> 0.32 us
    pallas_call x0 -> x13, Pallas kernels: none -> 519 us  [the longest x3 170 us: exchange(): pl.pallas_call(functools.partial(exchange_kernel, len(deep), len(flat), i...]
    all_gather x6 -> x2, waiting for transfers between devices: 248 us -> 0.04 us  [the longest x1 0.02 us: planar(): lax.all_gather(triple_turned.reshape(-1, triple_turned.shape[2]), 'z', ax...]
    reduce_scatter x6 -> x2, waiting for transfers between devices: 250 us -> 65.2 us  [the longest x1 57.9 us: planar(): lax.psum_scatter(expand_term, 'z', scatter_dimension=0, tiled=True)]
    unnamed x18 -> x8, waiting for transfers between devices: 126 us -> 1.98 us
    all_to_all x4 -> x0, blocking collectives: 106 us -> none  [the longest x1 56.2 us: spread_rows(): return lax.all_to_all(rows, 'z', split_axis=0, concat_axis=0, tiled=True)]
    all_gather x1 -> x0, blocking collectives: 103 us -> none  [planar(): lax.all_gather(jnp.concatenate(pieces), ('dp', 'z', 'y', 'x'), axis=0, ti...]
    reduce_scatter x1, waiting for transfers between devices: 76.5 us -> 1.46 us  [planar(): lax.psum_scatter(shrink_term, 'z', scatter_dimension=0, tiled=True)]
    reduce_scatter x1, waiting for transfers between devices: 55.1 us -> 0.01 us  [planar(): lax.psum_scatter(dense_wide, ('z', 'x'), scatter_dimension=0, tiled=True)]
  transfers between devices with their start and end apart: 21 -> 8, of which waited for: 14 -> 5; matrix products, arithmetic and copies ran while one was open for 19% -> 13% of each run, Pallas kernels for 0% -> 40%
where the time goes in v2:
time: 872 us; the launch traced here: 865 us
  Pallas kernels  519 us (60%)
  matrix products  133 us (15%)
  waiting for transfers between devices  130 us (15%)
  local copies, waits for them, and re-layouts  47.8 us (5%)
  other arithmetic  19.7 us (2%)
  between operations  15 us (2%)
    pallas_call x3, Pallas kernels, exchange(): pl.pallas_call(functools.partial(exchange_kernel, len(deep), len(flat), i...  170 us
    pallas_call x4, Pallas kernels, gather_tokens(): pl.pallas_call(gather_kernel, out_shape=jax.ShapeDtypeStruct((8, count, w...  159 us
    pallas_call x4, Pallas kernels, scatter_tokens(): pl.pallas_call(scatter_kernel, out_shape=jax.ShapeDtypeStruct((count, wid...  156 us
    all_gather x1, waiting for transfers between devices, planar(): shrink_own = lax.all_gather(shrink_weight, 'z', axis=0, tiled=True)  60.5 us
    reduce_scatter x1, waiting for transfers between devices, planar(): lax.psum_scatter(expand_term, 'z', scatter_dimension=0, tiled=True)  57.9 us
    dot_general x1, matrix products, planar(): jnp.einsum('tf,uf->tu', upstream_all, shrink_own, preferred_element_type=...  20.4 us
    unnamed x80, local copies, waits for them, and re-layouts  20.2 us
    pallas_call x1, Pallas kernels, attend_backward(): pl.pallas_call(functools.partial(backward_kernel, depth, seq_rows, block)...  19.2 us
  transfers between devices with their start and end apart: 8, of which 5 were waited for; matrix products, arithmetic and copies ran while one was open for 13% of the time, Pallas kernels for 40%

profile of v2, /device:TPU:10, one launch (start us, length us, event | category | flops | bytes accessed | tf_op | source)
XLA Modules:
  0.0 865.3 jit_solution(13662651883944883706)
XLA Ops:
  7.3 5.5 concatenate.6
  12.8 1.6 copy.33
  14.4 1.1 copy.34
  15.5 1.4 reshape.288.refs_2_
  18.9 1.1 copy-done.8
  20.0 1.2 copy-done.9
  21.2 1.2 copy-done.10
  22.4 52.3 %exchange_3.1 = (bf16[4,64,2048]{2,1,0:T(8,128)(2,1)S(1)}, bf16[4,64,2048]{2,1,0:T(8,128)(2,1)S(1)}, bf16[4,128,768]{2,1,0:T(8,128)(2,1)S(1)}, bf16[4,128,1024]{...) custom-call(bf16[4,64,2048]{2,1,0:T(8,128)(2,1)S(1)} %bitcast.126, bf16[4,64,2048]{2,1,0:T(8,128)(2,1)S(1)} %bitcast.127, ...), custom_call_target="tpu_custom_call" | custom-call | bytes 62980096 | tf_op jit(solution)/shard_map/exchange_3/pallas_call | solution.py:702
  74.8 1.0 copy-done.12
  75.7 0.9 copy-done.17
  78.8 0.9 convert_reduce_fusion.2
  81.7 1.4 fusion.13.rows_ref
  83.1 38.9 %gather_tokens.4 = bf16[8,256,2048]{2,1,0:T(8,128)(2,1)} custom-call(bf16[256,2048]{1,0:T(8,128)(2,1)} %fusion.13.rows_ref), custom_call_target="tpu_custom_call" | custom-call | bytes 33554432 | tf_op jit(solution)/shard_map/gather_tokens/pallas_call | solution.py:487
  122.1 41.9 %gather_tokens.6 = bf16[8,256,2048]{2,1,0:T(8,128)(2,1)} custom-call(bf16[256,2048]{1,0:T(8,128)(2,1)} %bitcast.120), custom_call_target="tpu_custom_call" | custom-call | bytes 33554432 | tf_op jit(solution)/shard_map/gather_tokens/pallas_call | solution.py:487
  164.2 10.2 %add_convert_fusion.item_ref = bf16[2048,768]{1,0:T(8,128)(2,1)S(1)} fusion(f32[768]{0:T(1024)S(1)} %add.168, bf16[2048,2048]{1,0:T(8,128)(2,1)} %bitcast.140, bf16[2048,768]{1,0:T(8,128)(2,1)} %all-gather.5.cloned.1.call-done), kind=kOutput, calls=%fused_computation.17 | convolution fusion | flops 6445596672 | bytes 14683136 | tf_op jit(solution)/shard_map/dot_general | solution.py:979
  174.4 13.6 %attend_forward.1 = (bf16[2048,256]{1,0:T(8,128)(2,1)S(1)}, f32[4,1,1024]{2,1,0:T(1,128)S(1)}) custom-call(s32[2]{0:T(128)S(1)} %fusion.25.prefix_ref, f32[2]{0:T(128)S(1)} %multiply_power_fusion.slope_ref, bf16[2048,768]{1,0:T(8,128)(2,1)S(1)} %add_convert_fusion.item_ref), custom_call_target="tpu_custom_call" | custom-call | flops 2147483648 | bytes 6291456 | tf_op jit(solution)/shard_map/attend_forward/pallas_call | solution.py:771
  188.0 1.6 copy-done.19
  189.6 1.0 all-gather.7.cloned.1.call-done
  190.7 3.6 convolution_convert_fusion.3
  194.3 39.1 %scatter_tokens.4 = f32[256,2048]{1,0:T(8,128)S(1)} custom-call(bf16[8,256,2048]{2,1,0:T(8,128)(2,1)S(1)} %bitcast.119), custom_call_target="tpu_custom_call" | custom-call | bytes 33554432 | tf_op jit(solution)/shard_map/scatter_tokens/pallas_call | solution.py:555
  234.1 0.9 copy-done.20
  235.1 1.4 add_convert_fusion.3.rows_ref
  236.5 39.6 %gather_tokens.5 = bf16[8,256,2048]{2,1,0:T(8,128)(2,1)} custom-call(bf16[256,2048]{1,0:T(8,128)(2,1)} %add_convert_fusion.3.rows_ref), custom_call_target="tpu_custom_call" | custom-call | bytes 33554432 | tf_op jit(solution)/shard_map/gather_tokens/pallas_call | solution.py:487
  276.1 14.6 %fusion.37 = f32[2048,1024]{1,0:T(8,128)} fusion(bf16[2048,2048]{1,0:T(8,128)(2,1)} %bitcast.144, bf16[2048,1024]{1,0:T(8,128)(2,1)} %all-gather.9.cloned.1.call-done), kind=kOutput, calls=%fused_computation.94 | convolution fusion | flops 8589934592 | bytes 20971520 | tf_op jit(solution)/shard_map/dot_general | solution.py:995
  290.8 60.5 %all-gather.11.cloned.1.call-done = bf16[1024,2048]{1,0:T(8,128)(2,1)} async-done(((bf16[256,2048]{1,0:T(8,128)(2,1)}), bf16[1024,2048]{1,0:T(8,128)(2,1)}) %all-gather.11.cloned.1.call-update) | async-done | bytes 4194320 | tf_op jit(solution)/shard_map/all_gather | solution.py:966
  351.2 13.4 %convolution_convert_fusion.2 = bf16[2048,2048]{1,0:T(8,128)(2,1)S(1)} fusion(bf16[1024,2048]{1,0:T(8,128)(2,1)} %all-gather.11.cloned.1.call-done, f32[2048,1024]{1,0:T(8,128)} %fusion.37, f32[1024]{0:T(1024)S(1)} %bitcast.154), kind=kOutput, calls=%fused_computation.14 | convolution fusion | flops 8615100416 | bytes 20975616 | tf_op jit(solution)/shard_map/dot_general | solution.py:998
  364.6 39.1 %scatter_tokens.5 = f32[256,2048]{1,0:T(8,128)S(1)} custom-call(bf16[8,256,2048]{2,1,0:T(8,128)(2,1)S(1)} %bitcast.123), custom_call_target="tpu_custom_call" | custom-call | bytes 33554432 | tf_op jit(solution)/shard_map/scatter_tokens/pallas_call | solution.py:555
  403.8 20.4 %convert_reduce_fusion = (f32[1024]{0:T(1024)S(1)}, bf16[2048,1024]{1,0:T(8,128)(2,1)S(1)}) fusion(f32[2048,1024]{1,0:T(8,128)} %fusion.37, f32[1024]{0:T(1024)S(1)} %bitcast.155, bf16[2048,2048]{1,0:T(8,128)(2,1)} %bitcast.138, bf16[1024,2048]{1,0:T(8,128)(2,1)} %all-gather.11.cloned.1.call-done), kind=kOutput, calls=%fused_computation.10 | convolution fusion | flops 8646556672 | bytes 25174016 | tf_op jit(solution)/shard_map/tf,uf->tu/dot_general | solution.py:1001
  424.2 9.6 %convolution_convert_fusion.1 = bf16[2048,2048]{1,0:T(8,128)(2,1)S(1)} fusion(bf16[2048,1024]{1,0:T(8,128)(2,1)S(1)} %get-tuple-element.72, bf16[2048,1024]{1,0:T(8,128)(2,1)S(1)} %copy-done.33), kind=kOutput, calls=%fused_computation.13 | convolution fusion | flops 8594128896 | bytes 16777216 | tf_op jit(solution)/shard_map/tu,du->td/dot_general | solution.py:1003
  433.8 38.9 %scatter_tokens.6 = f32[256,2048]{1,0:T(8,128)S(1)} custom-call(bf16[8,256,2048]{2,1,0:T(8,128)(2,1)S(1)} %bitcast.122), custom_call_target="tpu_custom_call" | custom-call | bytes 33554432 | tf_op jit(solution)/shard_map/scatter_tokens/pallas_call | solution.py:555
  472.7 0.8 multiply_reduce_fusion
  473.5 1.7 fusion.31
  475.2 1.6 convert_reduce_fusion.4
  476.9 38.8 %gather_tokens.7 = bf16[8,256,2048]{2,1,0:T(8,128)(2,1)} custom-call(bf16[256,2048]{1,0:T(8,128)(2,1)} %get-tuple-element.74.rows_ref), custom_call_target="tpu_custom_call" | custom-call | bytes 33554432 | tf_op jit(solution)/shard_map/gather_tokens/pallas_call | solution.py:487
  515.7 1.6 broadcast_in_dim.52
  517.2 6.7 fusion.6
  524.0 6.2 convolution_convert_fusion.8.grad_ref
  530.2 19.2 %attend_backward.1 = bf16[2048,768]{1,0:T(8,128)(2,1)S(1)} custom-call(s32[2]{0:T(128)S(1)} %fusion.25.prefix_ref, f32[2]{0:T(128)S(1)} %multiply_power_fusion.slope_ref, bf16[2048,768]{1,0:T(8,128)(2,1)} %copy-done.19, bf16[2048,256]{1,0:T(8,128)(2,1)S(1)} %convolution_convert_fusion.8.grad_ref, f32[4,1,1024]{2,1,0:T(1,128)S(1)} %get-tuple-element.31.total_ref), custom_call_target="tpu_custom_call" | custom-call | flops 5368709120 | bytes 6291456 | tf_op jit(solution)/shard_map/attend_backward/pallas_call | solution.py:847
  549.5 8.5 convolution_convert_fusion.6
  558.0 14.4 %convolution_convert_fusion.5 = bf16[2048,1024]{1,0:T(8,128)(2,1)} fusion(bf16[2048,2048]{1,0:T(8,128)(2,1)} %bitcast.145, bf16[2048,1024]{1,0:T(8,128)(2,1)} %copy-done.34), kind=kOutput, calls=%fused_computation.19 | convolution fusion | flops 8592031744 | bytes 16777216 | tf_op jit(solution)/shard_map/td,tu->du/dot_general | solution.py:1014
  572.5 16.5 %convolution_convert_fusion.4 = bf16[1024,2048]{1,0:T(8,128)(2,1)} fusion(bf16[2048,2048]{1,0:T(8,128)(2,1)} %bitcast.139, f32[2048,1024]{1,0:T(8,128)} %fusion.37, f32[1024]{0:T(1024)S(1)} %bitcast.156), kind=kOutput, calls=%fused_computation.18 | convolution fusion | flops 8613003264 | bytes 20975616 | tf_op jit(solution)/shard_map/tu,td->ud/dot_general | solution.py:1010
  590.6 9.4 %convolution_convert_fusion = bf16[2048,2048]{1,0:T(8,128)(2,1)S(1)} fusion(bf16[2048,768]{1,0:T(8,128)(2,1)S(1)} %attend_backward.1, bf16[2048,768]{1,0:T(8,128)(2,1)} %all-gather.5.cloned.1.call-done), kind=kOutput, calls=%fused_computation.12 | convolution fusion | flops 6446645248 | bytes 14680064 | tf_op jit(solution)/shard_map/tc,dc->td/dot_general | solution.py:1039
  600.0 39.3 %scatter_tokens.7 = f32[256,2048]{1,0:T(8,128)S(1)} custom-call(bf16[8,256,2048]{2,1,0:T(8,128)(2,1)S(1)} %bitcast.121), custom_call_target="tpu_custom_call" | custom-call | bytes 33554432 | tf_op jit(solution)/shard_map/scatter_tokens/pallas_call | solution.py:555
  640.0 0.9 fusion.14
  641.2 3.9 add_convert_fusion.1
  645.1 1.8 convert_element_type.233
  646.9 7.3 reduce-scatter.7.cloned.1.call-done
  654.2 1.1 copy-done.18
  655.3 11.8 %exchange_5.1 = bf16[4,128,768]{2,1,0:T(8,128)(2,1)S(1)} custom-call(bf16[4,128,768]{2,1,0:T(8,128)(2,1)S(1)} %bitcast.133), custom_call_target="tpu_custom_call" | custom-call | bytes 12582912 | tf_op jit(solution)/shard_map/exchange_5/pallas_call | solution.py:702
  667.1 2.0 reshape.331
  669.1 3.8 copy.39
  672.8 3.0 copy.43
  675.9 57.9 %reduce-scatter.5.cloned.1.call-done = bf16[512,1024]{1,0:T(8,128)(2,1)} async-done(((bf16[2048,1024]{1,0:T(8,128)(2,1)}), bf16[512,1024]{1,0:T(8,128)(2,1)}) %reduce-scatter.5.cloned.1.call-update) | async-done | bytes 1048592 | tf_op jit(solution)/shard_map/reduce_scatter | solution.py:1017
  733.8 1.2 copy-done.11
  735.0 106.4 %exchange_4.1 = (bf16[4,64,2048]{2,1,0:T(8,128)(2,1)S(1)}, bf16[4,64,2048]{2,1,0:T(8,128)(2,1)S(1)}, bf16[4,128,1024]{2,1,0:T(8,128)(2,1)S(1)}, f32[8,128]{1,0:T(8,128)S(1)}) custom-call(bf16[4,64,2048]{2,1,0:T(8,128)(2,1)S(1)} %bitcast.124, bf16[4,64,2048]{2,1,0:T(8,128)(2,1)S(1)} %bitcast.125, bf16[4,128,1024]{2,1,0:T(8,128)(2,1)S(1)} %bitcast.128, ...), custom_call_target="tpu_custom_call" | custom-call | bytes 52428800 | tf_op jit(solution)/shard_map/exchange_4/pallas_call | solution.py:702
  841.4 1.0 copy-done.13
  842.4 1.0 copy-done.15
  843.3 0.9 reshape.332
  844.3 2.7 copy.40
  847.0 3.4 reshape.330
  852.1 1.5 reduce-scatter.11.cloned.1.call-done
  853.5 2.8 convert_element_type.239
  856.3 1.0 copy.54
  857.3 1.0 copy.55
  (144 shorter events, 11.4 us)
Async XLA Ops:
  7.2 156.8 %copy-start = (s32[4,2]{0,1:T(2,128)S(1)}, s32[4,2]{0,1:T(2,128)}, u32[]{:S(2)}) copy-start(s32[4,2]{0,1:T(2,128)} %param.16) | copy-start | bytes 100
  7.2 9.7 %copy-start.23 = (bf16[128,4096]{1,0:T(8,128)(2,1)S(1)}, bf16[128,4096]{1,0:T(8,128)(2,1)}, u32[]{:S(2)}) copy-start(bf16[128,4096]{1,0:T(8,128)(2,1)} %param.26) | copy-start | bytes 3145732
  7.2 157.0 %all-gather.5.cloned.1.call-start = ((), (), s32[]{:S(2)}) async-start(), calls=%async_computation.4 | async-start | bytes 3932160 | tf_op jit(solution)/shard_map/all_gather | solution.py:960
  18.8 1.1 copy-start.8
  20.0 1.2 copy-start.9
  21.2 1.2 copy-start.10
  74.8 1.0 copy-start.12
  75.7 0.9 copy-start.17
  76.6 3.6 copy-start.4
  76.6 156.7 %copy-start.2 = (bf16[4,64,2048]{2,1,0:T(8,128)(2,1)}, bf16[4,64,2048]{2,1,0:T(8,128)(2,1)S(1)}, u32[]{:S(2)}) copy-start(bf16[4,64,2048]{2,1,0:T(8,128)(2,1)S(1)} %get-tuple-element.25) | copy-start | bytes 3145732
  76.7 114.0 %all-gather.7.cloned.1.call-start = ((), (), s32[]{:S(2)}) async-start(), calls=%async_computation.5 | async-start | bytes 2359296 | tf_op jit(solution)/shard_map/all_gather | solution.py:967
  77.4 198.7 %all-gather.9.cloned.1.call-start = ((), (), s32[]{:S(2)}) async-start(), calls=%async_computation.6 | async-start | bytes 5242880 | tf_op jit(solution)/shard_map/all_gather | solution.py:963
  78.1 273.1 %all-gather.11.cloned.1.call-start = ((), (), s32[]{:S(2)}) async-start(), calls=%async_computation.7 | async-start | bytes 5242880 | tf_op jit(solution)/shard_map/all_gather | solution.py:966
  78.7 566.4 %reduce-scatter.9.cloned.1.call-start = ((), (), s32[]{:S(2)}) async-start(), calls=%async_computation.10 | async-start | bytes 2359296 | tf_op jit(solution)/shard_map/reduce_scatter | solution.py:1025
  79.8 42.3 %copy-start.27 = (f32[256]{0:T(256)}, f32[256]{0:T(256)S(1)}, u32[]{:S(2)}) copy-start(f32[256]{0:T(256)S(1)} %div.48) | copy-start | bytes 3076
  80.7 0.6 copy-start.31
  80.7 41.3 %copy-start.29 = (f32[256]{0:T(256)}, f32[256]{0:T(256)S(1)}, u32[]{:S(2)}) copy-start(f32[256]{0:T(256)S(1)} %rsqrt.21) | copy-start | bytes 3076
  81.4 40.7 %copy-start.24 = (f32[2048]{0:T(1024)}, f32[2048]{0:T(1024)S(1)}, u32[]{:S(2)}) copy-start(f32[2048]{0:T(1024)S(1)} %reshape.321) | copy-start | bytes 24580
  188.0 1.6 copy-start.19
  233.7 1.3 copy-start.20
  403.8 20.4 %copy-start.33 = (bf16[2048,1024]{1,0:T(8,128)(2,1)S(1)}, bf16[2048,1024]{1,0:T(8,128)(2,1)}, u32[]{:S(2)}) copy-start(bf16[2048,1024]{1,0:T(8,128)(2,1)} %all-gather.9.cloned.1.call-done) | copy-start | bytes 12582916
  424.2 9.6 %copy-start.34 = (bf16[2048,1024]{1,0:T(8,128)(2,1)}, bf16[2048,1024]{1,0:T(8,128)(2,1)S(1)}, u32[]{:S(2)}) copy-start(bf16[2048,1024]{1,0:T(8,128)(2,1)S(1)} %get-tuple-element.72) | copy-start | bytes 12582916
  433.8 38.9 %copy-start.21 = (f32[256,2048]{1,0:T(8,128)S(1)}, f32[256,2048]{1,0:T(8,128)}, u32[]{:S(2)}) copy-start(f32[256,2048]{1,0:T(8,128)} %copy-done.20) | copy-start | bytes 6291460
  473.5 1.7 copy-start.5
  475.2 1.7 copy-start.22
  524.0 130.2 %reduce-scatter.7.cloned.1.call-start = ((), (), s32[]{:S(2)}) async-start(), calls=%async_computation.9 | async-start | bytes 3932160 | tf_op jit(solution)/shard_map/reduce_scatter | solution.py:1049
  524.0 25.4 %slice-start = ((s8[8388608]{0:T(1024)(128)(4,1)}), s8[4194304]{0:T(1024)(128)(4,1)S(1)}, s32[]{:S(2)}) async-start(s8[8388608]{0:T(1024)(128)(4,1)} %bitcast.141), calls=%async_computation.12 | async-start | bytes 8388608
  530.2 19.3 %slice-start.1 = ((s8[8388608]{0:T(1024)(128)(4,1)}), s8[4194304]{0:T(1024)(128)(4,1)S(1)}, s32[]{:S(2)}) async-start(s8[8388608]{0:T(1024)(128)(4,1)} %bitcast.141), calls=%async_computation.13 | async-start | bytes 8388608
  558.0 175.8 %reduce-scatter.5.cloned.1.call-start = ((), (), s32[]{:S(2)}) async-start(), calls=%async_computation.8 | async-start | bytes 5242880 | tf_op jit(solution)/shard_map/reduce_scatter | solution.py:1017
  572.5 281.1 %reduce-scatter.11.cloned.1.call-start = ((), (), s32[]{:S(2)}) async-start(), calls=%async_computation.11 | async-start | bytes 5242880 | tf_op jit(solution)/shard_map/reduce_scatter | solution.py:1013
  589.0 0.7 copy-start.26
  599.9 39.3 %copy-start.3 = (bf16[4,64,2048]{2,1,0:T(8,128)(2,1)S(1)}, bf16[4,64,2048]{2,1,0:T(8,128)(2,1)}, u32[]{:S(2)}) copy-start(bf16[4,64,2048]{2,1,0:T(8,128)(2,1)} %copy-done.2) | copy-start | bytes 3145732
  599.9 39.3 %copy-start.25 = (f32[2048]{0:T(1024)S(1)}, f32[2048]{0:T(1024)}, u32[]{:S(2)}) copy-start(f32[2048]{0:T(1024)} %copy-done.24) | copy-start | bytes 24580
  599.9 39.3 %copy-start.28 = (f32[256]{0:T(256)S(1)}, f32[256]{0:T(256)}, u32[]{:S(2)}) copy-start(f32[256]{0:T(256)} %copy-done.27) | copy-start | bytes 3076
  639.3 0.7 copy-start.32
  639.3 0.7 copy-start.30
  654.2 1.1 copy-start.18
  669.1 64.7 %copy-start.6 = (bf16[256,2048]{1,0:T(8,128)(2,1)S(1)}, bf16[256,2048]{1,0:T(8,128)(2,1)}, u32[]{:S(2)}) copy-start(bf16[256,2048]{1,0:T(8,128)(2,1)} %get-tuple-element.79) | copy-start | bytes 3145732
  669.1 64.7 %copy-start.7 = (bf16[256,2048]{1,0:T(8,128)(2,1)S(1)}, bf16[256,2048]{1,0:T(8,128)(2,1)}, u32[]{:S(2)}) copy-start(bf16[256,2048]{1,0:T(8,128)(2,1)} %add_convert_fusion.1) | copy-start | bytes 3145732
  733.8 1.2 copy-start.11
  841.4 1.0 copy-start.13
  842.4 1.0 copy-start.15
  847.0 9.3 %copy-start.16 = (bf16[4,64,2048]{2,1,0:T(8,128)(2,1)S(1)}, bf16[4,64,2048]{2,1,0:T(8,128)(2,1)}, u32[]{:S(2)}) copy-start(bf16[4,64,2048]{2,1,0:T(8,128)(2,1)} %copy-done.15) | copy-start | bytes 3145732
  850.4 6.9 copy-start.14
  851.5 6.8 copy-start.1
Sparse Core Ops, SparseCore 0:
  76.8 61.5 all-gather.4
  140.5 50.1 all-gather.6
  192.8 77.6 all-gather.8
  272.0 79.2 all-gather.10
  524.1 68.5 reduce-scatter.8
  594.8 59.2 reduce-scatter.6
  656.5 77.2 reduce-scatter.4
  736.1 117.3 reduce-scatter.10
